TPU v7x, 32 devices: a whole 2x2x4 slice. The times are simulated.
32 devices in a mesh: ty: 4 (over z), tx: 8 (over y, x, core).
Axes of the slice: x: 2, y: 2, z: 4, core: 2. Of those that a mesh axis runs over, the one named last changes fastest.
Arguments:
- x_tok: bfloat16 [8192, 1024], P('ty', 'tx')
- dy_tok: bfloat16 [8192, 1024], P('ty', 'tx')
- ln_gain: float32 [1024], P('tx')
- w_gate: bfloat16 [1024, 4096], P('tx', 'ty')
- w_up: bfloat16 [1024, 4096], P('tx', 'ty')
- w_down: bfloat16 [4096, 1024], P('ty', 'tx')
Outputs:
- output 1: bfloat16 [8192, 1024], P('ty', 'tx')
- output 2: bfloat16 [8192, 1024], P('ty', 'tx')
- output 3: float32 [1024, 4096], P('tx', 'ty')
- output 4: float32 [1024, 4096], P('tx', 'ty')
- output 5: float32 [4096, 1024], P('ty', 'tx')
- output 6: float32 [1024], P('tx')
All inputs are finite; a program needn't handle non-finite values.
Results may differ from a plain program's by a relative error of at most 0.001.
Values are sent between devices in bfloat16 or wider.
A program may use at most 1 GiB of HBM per device.

v0:
```python
import jax
import jax.numpy as jnp
from jax import lax
from jax.sharding import PartitionSpec as P

LN_EPS = 1e-6


def contract_rows(left_op, right_op):
    return lax.dot_general(left_op, right_op, (((0,), (0,)), ((), ())), preferred_element_type=jnp.float32)


def contract_cols(left_op, right_op):
    return lax.dot_general(left_op, right_op, (((1,), (1,)), ((), ())), preferred_element_type=jnp.float32)


def solution(mesh):
    tx_size = mesh.shape["tx"]

    def local_step(x_blk, dy_blk, gain_blk, w_gate_blk, w_up_blk, w_down_blk):
        d_model = x_blk.shape[1] * tx_size
        x_float = x_blk.astype(jnp.float32)
        ln_stats = lax.psum(jnp.stack([jnp.sum(x_float, axis=1), jnp.sum(x_float * x_float, axis=1)]), "tx") / d_model
        mean_x = ln_stats[0][:, None]
        inv_std = lax.rsqrt(ln_stats[1][:, None] - mean_x * mean_x + LN_EPS)
        x_hat = (x_float - mean_x) * inv_std
        h_blk = (gain_blk * x_hat).astype(jnp.bfloat16)
        h_all = lax.all_gather(h_blk, "ty", axis=0, tiled=True)
        gate_pre = lax.psum_scatter(jnp.dot(h_all, w_gate_blk, preferred_element_type=jnp.float32),
                                    "tx", scatter_dimension=0, tiled=True)
        up_pre = lax.psum_scatter(jnp.dot(h_all, w_up_blk, preferred_element_type=jnp.float32),
                                  "tx", scatter_dimension=0, tiled=True)
        gate_sig = jax.nn.sigmoid(gate_pre)
        gate_swish = gate_pre * gate_sig
        act_blk = (gate_swish * up_pre).astype(jnp.bfloat16)
        act_all = lax.all_gather(act_blk, "tx", axis=0, tiled=True)
        mlp_out = lax.psum_scatter(jnp.dot(act_all, w_down_blk, preferred_element_type=jnp.float32),
                                   "ty", scatter_dimension=0, tiled=True)
        y_blk = (x_float + mlp_out).astype(jnp.bfloat16)

        dy_all = lax.all_gather(dy_blk, "ty", axis=0, tiled=True)
        dw_down_blk = contract_rows(act_all, dy_all)
        d_act = lax.psum_scatter(contract_cols(dy_all, w_down_blk), "tx", scatter_dimension=0, tiled=True)
        d_gate = (d_act * up_pre * gate_sig * (1.0 + gate_pre * (1.0 - gate_sig))).astype(jnp.bfloat16)
        d_up = (d_act * gate_swish).astype(jnp.bfloat16)
        d_gate_all = lax.all_gather(d_gate, "tx", axis=0, tiled=True)
        d_up_all = lax.all_gather(d_up, "tx", axis=0, tiled=True)
        dw_gate_blk = contract_rows(h_all, d_gate_all)
        dw_up_blk = contract_rows(h_all, d_up_all)
        d_hnorm = lax.psum_scatter(contract_cols(d_gate_all, w_gate_blk) + contract_cols(d_up_all, w_up_blk),
                                   "ty", scatter_dimension=0, tiled=True)
        value_a6 = d_hnorm * gain_blk
        bwd_stats = lax.psum(jnp.stack([jnp.sum(value_a6, axis=1), jnp.sum(value_a6 * x_hat, axis=1)]), "tx") / d_model
        dx_ln = inv_std * (value_a6 - bwd_stats[0][:, None] - x_hat * bwd_stats[1][:, None])
        dx_blk = (dy_blk.astype(jnp.float32) + dx_ln).astype(jnp.bfloat16)
        d_gain_blk = lax.psum(jnp.sum(d_hnorm * x_hat, axis=0), "ty")
        return (y_blk, dx_blk, dw_gate_blk, dw_up_blk, dw_down_blk, d_gain_blk)

    return jax.shard_map(
        local_step, mesh=mesh,
        in_specs=(P("ty", "tx"), P("ty", "tx"), P("tx"), P("tx", "ty"), P("tx", "ty"), P("ty", "tx")),
        out_specs=(P("ty", "tx"), P("ty", "tx"), P("tx", "ty"), P("tx", "ty"), P("ty", "tx"), P("tx")),
        check_vma=False)
```

profile of v0, /device:TPU:0, one launch (start us, length us, event | category | flops | bytes accessed | tf_op | source)
XLA Modules:
  0.0 1201.7 jit_solution(9090436191548695802)
XLA Ops:
  7.2 1.6 convert_reduce_fusion
  8.8 25.6 %psum.21 = f32[2,2048]{1,0:T(2,128)S(1)} all-reduce(f32[2,2048]{1,0:T(2,128)S(1)} %pad_maximum_fusion), channel_id=1, replica_groups=mesh['ty'=4,'tx'=8] {'tx'}, use_global_device_ids=true, to_apply=%region_2.0 | all-reduce | flops 4096 | bytes 32768 | tf_op jit(solution)/shard_map/psum | solution.py:23
  34.4 2.4 fusion.7
  37.0 0.7 all-gather.10.cloned.1.call-update
  37.7 44.0 %all-gather.6.cloned.1.call-done = bf16[8192,128]{1,0:T(8,128)(2,1)} async-done(((bf16[2048,128]{1,0:T(8,128)(2,1)}), bf16[8192,128]{1,0:T(8,128)(2,1)}) %all-gather.6.cloned.1.call-update) | async-done | bytes 2097168 | tf_op jit(solution)/shard_map/all_gather | solution.py:28
  81.7 17.2 %fusion.18 = f32[8192,1024]{1,0:T(8,128)} fusion(bf16[8192,128]{1,0:T(8,128)(2,1)} %all-gather.6.cloned.1.call-done, bf16[128,1024]{1,0:T(8,128)(2,1)} %param.10), kind=kOutput, calls=%fused_computation.33 | convolution fusion | flops 2147483648 | bytes 35913728 | tf_op jit(solution)/shard_map/dot_general | solution.py:31
  99.0 1.5 copy-done.1
  100.5 13.1 %fusion.17 = f32[8192,1024]{1,0:T(8,128)} fusion(bf16[8192,128]{1,0:T(8,128)(2,1)S(1)} %copy-done.1, bf16[128,1024]{1,0:T(8,128)(2,1)S(1)} %copy-done), kind=kOutput, calls=%fused_computation.32 | convolution fusion | flops 2147483648 | bytes 35913728 | tf_op jit(solution)/shard_map/dot_general | solution.py:29
  113.6 14.0 %all-gather.10.cloned.1.call-done = bf16[8192,128]{1,0:T(8,128)(2,1)} async-done(((bf16[2048,128]{1,0:T(8,128)(2,1)}), bf16[8192,128]{1,0:T(8,128)(2,1)}) %all-gather.10.cloned.1.call-update) | async-done | bytes 2097168 | tf_op jit(solution)/shard_map/all_gather | solution.py:41
  127.6 14.7 %fusion.20 = f32[8192,1024]{1,0:T(8,128)} fusion(bf16[8192,128]{1,0:T(8,128)(2,1)} %all-gather.10.cloned.1.call-done, bf16[1024,128]{1,0:T(8,128)(2,1)S(1)} %copy-done.6), kind=kOutput, calls=%fused_computation.35 | convolution fusion | flops 2147483648 | bytes 35913728 | tf_op jit(solution)/shard_map/dot_general | solution.py:14
  142.6 192.2 %reduce-scatter.8.cloned.1.call-done = f32[1024,1024]{1,0:T(8,128)} async-done(((f32[8192,1024]{1,0:T(8,128)}), f32[1024,1024]{1,0:T(8,128)}) %reduce-scatter.8.cloned.1.call-update) | async-done | bytes 4194320 | tf_op jit(solution)/shard_map/reduce_scatter | solution.py:31
  334.8 208.0 %reduce-scatter.6.cloned.1.call-done = f32[1024,1024]{1,0:T(8,128)} async-done(((f32[8192,1024]{1,0:T(8,128)}), f32[1024,1024]{1,0:T(8,128)}) %reduce-scatter.6.cloned.1.call-update) | async-done | bytes 4194320 | tf_op jit(solution)/shard_map/reduce_scatter | solution.py:29
  542.8 208.0 %reduce-scatter.12.cloned.1.call-done = f32[1024,1024]{1,0:T(8,128)} async-done(((f32[8192,1024]{1,0:T(8,128)}), f32[1024,1024]{1,0:T(8,128)}) %reduce-scatter.12.cloned.1.call-update) | async-done | bytes 4194320 | tf_op jit(solution)/shard_map/reduce_scatter | solution.py:43
  750.8 8.5 multiply_convert_fusion
  759.4 0.7 all-gather.14.cloned.1.call-update
  760.2 0.7 all-gather.8.cloned.1.call-update
  760.9 88.2 %all-gather.12.cloned.1.call-done = bf16[8192,1024]{1,0:T(8,128)(2,1)} async-done(((bf16[1024,1024]{1,0:T(8,128)(2,1)}), bf16[8192,1024]{1,0:T(8,128)(2,1)}) %all-gather.12.cloned.1.call-update) | async-done | bytes 16777232 | tf_op jit(solution)/shard_map/all_gather | solution.py:46
  849.2 10.1 fusion.21
  859.2 81.5 %all-gather.14.cloned.1.call-done = bf16[8192,1024]{1,0:T(8,128)(2,1)} async-done(((bf16[1024,1024]{1,0:T(8,128)(2,1)}), bf16[8192,1024]{1,0:T(8,128)(2,1)}) %all-gather.14.cloned.1.call-update) | async-done | bytes 16777232 | tf_op jit(solution)/shard_map/all_gather | solution.py:47
  940.7 11.7 convolution_add_fusion
  952.4 0.3 reduce-scatter.10.cloned.1.call-start
  952.7 79.6 %all-gather.8.cloned.1.call-done = bf16[8192,1024]{1,0:T(8,128)(2,1)} async-done(((bf16[1024,1024]{1,0:T(8,128)(2,1)}), bf16[8192,1024]{1,0:T(8,128)(2,1)}) %all-gather.8.cloned.1.call-update) | async-done | bytes 16777232 | tf_op jit(solution)/shard_map/all_gather | solution.py:36
  1032.3 10.2 fusion.19
  1042.5 9.1 fusion.22
  1051.6 9.1 fusion.23
  1060.7 5.3 fusion.24
  1066.0 45.3 %reduce-scatter.14.cloned.1.call-done = f32[2048,128]{1,0:T(8,128)} async-done(((f32[8192,128]{1,0:T(8,128)}), f32[2048,128]{1,0:T(8,128)}) %reduce-scatter.14.cloned.1.call-update) | async-done | bytes 1048592 | tf_op jit(solution)/shard_map/reduce_scatter | solution.py:50
  1111.3 2.3 fusion.13
  1113.6 11.7 psum.23
  1125.3 22.5 %psum.22 = f32[2,2048]{1,0:T(2,128)S(1)} all-reduce(f32[2,2048]{1,0:T(2,128)S(1)} %pad_maximum_fusion.1), channel_id=1, replica_groups=mesh['ty'=4,'tx'=8] {'tx'}, use_global_device_ids=true, to_apply=%region_10.0 | all-reduce | flops 4096 | bytes 32768 | tf_op jit(solution)/shard_map/psum | solution.py:53
  1147.8 42.9 %reduce-scatter.10.cloned.1.call-done = f32[2048,128]{1,0:T(8,128)} async-done(((f32[8192,128]{1,0:T(8,128)}), f32[2048,128]{1,0:T(8,128)}) %reduce-scatter.10.cloned.1.call-update) | async-done | bytes 1048592 | tf_op jit(solution)/shard_map/reduce_scatter | solution.py:37
  1190.7 4.1 fusion.12
  (47 shorter events, 0.8 us)
Async XLA Ops:
  7.2 91.8 %copy-start = (bf16[128,1024]{1,0:T(8,128)(2,1)S(1)}, bf16[128,1024]{1,0:T(8,128)(2,1)}, u32[]{:S(2)}) copy-start(bf16[128,1024]{1,0:T(8,128)(2,1)} %param.9) | copy-start | bytes 786436
  7.2 74.5 %all-gather.6.cloned.1.call-start = ((), (), s32[]{:S(2)}) async-start(), calls=%async_computation.5 | async-start | bytes 2621440 | tf_op jit(solution)/shard_map/all_gather | solution.py:28
  36.9 90.7 %all-gather.10.cloned.1.call-start = ((), (), s32[]{:S(2)}) async-start(), calls=%async_computation.10 | async-start | bytes 2621440 | tf_op jit(solution)/shard_map/all_gather | solution.py:41
  37.7 297.1 %reduce-scatter.8.cloned.1.call-start = ((), (), s32[]{:S(2)}) async-start(), calls=%async_computation.7 | async-start | bytes 37748736 | tf_op jit(solution)/shard_map/reduce_scatter | solution.py:31
  98.9 1.6 copy-start.1
  98.9 443.9 %reduce-scatter.6.cloned.1.call-start = ((), (), s32[]{:S(2)}) async-start(), calls=%async_computation.6 | async-start | bytes 37748736 | tf_op jit(solution)/shard_map/reduce_scatter | solution.py:29
  113.5 14.1 %copy-start.6 = (bf16[1024,128]{1,0:T(8,128)(2,1)S(1)}, bf16[1024,128]{1,0:T(8,128)(2,1)}, u32[]{:S(2)}) copy-start(bf16[1024,128]{1,0:T(8,128)(2,1)} %param.11) | copy-start | bytes 786436
  113.6 637.2 %reduce-scatter.12.cloned.1.call-start = ((), (), s32[]{:S(2)}) async-start(), calls=%async_computation.11 | async-start | bytes 37748736 | tf_op jit(solution)/shard_map/reduce_scatter | solution.py:43
  142.4 706.8 %all-gather.12.cloned.1.call-start = ((), (), s32[]{:S(2)}) async-start(), calls=%async_computation.12 | async-start | bytes 18874368 | tf_op jit(solution)/shard_map/all_gather | solution.py:46
  759.4 181.3 %all-gather.14.cloned.1.call-start = ((), (), s32[]{:S(2)}) async-start(), calls=%async_computation.13 | async-start | bytes 18874368 | tf_op jit(solution)/shard_map/all_gather | solution.py:47
  760.1 272.1 %all-gather.8.cloned.1.call-start = ((), (), s32[]{:S(2)}) async-start(), calls=%async_computation.8 | async-start | bytes 18874368 | tf_op jit(solution)/shard_map/all_gather | solution.py:36
  760.9 179.8 %copy-start.5 = (bf16[128,1024]{1,0:T(8,128)(2,1)S(1)}, bf16[128,1024]{1,0:T(8,128)(2,1)}, u32[]{:S(2)}) copy-start(bf16[128,1024]{1,0:T(8,128)(2,1)} %param.10) | copy-start | bytes 786436
  760.9 350.4 %reduce-scatter.14.cloned.1.call-start = ((), (), s32[]{:S(2)}) async-start(), calls=%async_computation.14 | async-start | bytes 5242880 | tf_op jit(solution)/shard_map/reduce_scatter | solution.py:50
  952.4 238.3 %reduce-scatter.10.cloned.1.call-start = ((), (), s32[]{:S(2)}) async-start(), calls=%async_computation.9 | async-start | bytes 5242880 | tf_op jit(solution)/shard_map/reduce_scatter | solution.py:37
  1042.5 18.2 %slice-start = ((s8[16777216]{0:T(1024)(128)(4,1)}), s8[4194304]{0:T(1024)(128)(4,1)S(1)}, s32[]{:S(2)}) async-start(s8[16777216]{0:T(1024)(128)(4,1)} %bitcast.26), calls=%async_computation.15 | async-start | bytes 8388608
  1042.5 18.2 %slice-start.1 = ((s8[16777216]{0:T(1024)(128)(4,1)}), s8[4194304]{0:T(1024)(128)(4,1)S(1)}, s32[]{:S(2)}) async-start(s8[16777216]{0:T(1024)(128)(4,1)} %bitcast.26), calls=%async_computation.16 | async-start | bytes 8388608
  1051.6 9.1 slice-start.2
  1051.6 9.1 slice-start.3
  1051.6 9.1 copy-start.3
  1060.7 50.6 %copy-start.2 = (bf16[2048,128]{1,0:T(8,128)(2,1)S(1)}, bf16[2048,128]{1,0:T(8,128)(2,1)}, u32[]{:S(2)}) copy-start(bf16[2048,128]{1,0:T(8,128)(2,1)} %param.6) | copy-start | bytes 1572868
  1060.7 50.6 %copy-start.7 = (f32[128]{0:T(128)S(1)}, f32[128]{0:T(128)}, u32[]{:S(2)}) copy-start(f32[128]{0:T(128)} %param.8) | copy-start | bytes 1540
  1060.7 130.0 %copy-start.4 = (bf16[2048,128]{1,0:T(8,128)(2,1)S(1)}, bf16[2048,128]{1,0:T(8,128)(2,1)}, u32[]{:S(2)}) copy-start(bf16[2048,128]{1,0:T(8,128)(2,1)} %param.7) | copy-start | bytes 1572868
Sparse Core Ops, SparseCore 0:
  37.0 44.6 all-gather.5
  83.3 44.2 all-gather.9
  131.2 203.5 reduce-scatter.7
  338.2 204.5 reduce-scatter.5
  546.2 204.5 reduce-scatter.11
  759.5 89.6 all-gather.11
  851.0 89.6 all-gather.13
  942.6 89.6 all-gather.7
  1034.6 76.6 reduce-scatter.13
  1113.4 77.2 reduce-scatter.9
where the time goes:
time: 1200 us
  waiting for transfers between devices  1010 us (84%)
  matrix products  100 us (8%)
  blocking collectives  59.7 us (5%)
  other arithmetic  19.1 us (2%)
  between operations  14.3 us (1%)
    reduce_scatter x1, waiting for transfers between devices, local_step(): lax.psum_scatter(contract_cols(dy_all, w_down_blk), 'tx', scatter_dimensi...  208 us
    reduce_scatter x1, waiting for transfers between devices, local_step(): lax.psum_scatter(jnp.dot(h_all, w_gate_blk, preferred_element_type=jnp.fl...  208 us
    reduce_scatter x1, waiting for transfers between devices, local_step(): lax.psum_scatter(jnp.dot(h_all, w_up_blk, preferred_element_type=jnp.floa...  192 us
    all_gather x1, waiting for transfers between devices, local_step(): d_gate_all = lax.all_gather(d_gate, 'tx', axis=0, tiled=True)  88.2 us
    all_gather x1, waiting for transfers between devices, local_step(): d_up_all = lax.all_gather(d_up, 'tx', axis=0, tiled=True)  81.5 us
    all_gather x1, waiting for transfers between devices, local_step(): act_all = lax.all_gather(act_blk, 'tx', axis=0, tiled=True)  79.6 us
    reduce_scatter x1, waiting for transfers between devices, local_step(): lax.psum_scatter(contract_cols(d_gate_all, w_gate_blk) + contract_cols(d_...  45.3 us
    all_gather x1, waiting for transfers between devices, local_step(): h_all = lax.all_gather(h_blk, 'ty', axis=0, tiled=True)  44 us
  transfers between devices with their start and end apart: 10, of which 10 were waited for; matrix products, arithmetic and copies ran while one was open for 9% of the time, Pallas kernels for 0%

commit v1 on v0

v1 whole, which is shorter than its diff:
```python
import functools

import jax
import jax.numpy as jnp
from jax import lax
from jax.experimental import pallas as pl
from jax.experimental.pallas import tpu as pltpu
from jax.sharding import PartitionSpec as P

LN_EPS = 1e-6
F32 = jnp.float32
BF16 = jnp.bfloat16
MESH = pl.DeviceIdType.MESH
LANE = 128


def place():
    z = lax.axis_index("ty")
    t = lax.axis_index("tx")
    core = lax.rem(t, 2)
    xbit = lax.rem(lax.div(t, 2), 2)
    ybit = lax.div(t, 4)
    flips = (1 - 2 * core, 2 - 4 * xbit, 4 - 8 * ybit)

    def peer(s):
        out = t
        for bit in range(3):
            if s >> bit & 1:
                out = out + flips[bit]
        return out

    return z, t, peer


def cols(k, width=LANE):
    return pl.ds(pl.multiple_of(k * width, width), width)


class Sends:
    def __init__(self, send_sem, recv_sem):
        self.send_sem, self.recv_sem, self.count, self.started = send_sem, recv_sem, 0, []

    def slot(self):
        self.count += 1
        return self.count - 1

    def copy(self, src, dst, slot, device):
        return pltpu.make_async_remote_copy(src_ref=src, dst_ref=dst, send_sem=self.send_sem.at[slot],
                                            recv_sem=self.recv_sem.at[slot], device_id=device, device_id_type=MESH)


def gather_kernel(x_in, dy_in, g_in, w1_in, w3_in, w2_in,
                  h_out, dy_all, x_rows, gain_all, w1_all, w3_all, w2_all,
                  x_all, send_sem, recv_sem, local_sem):
    z, t, peer = place()
    tokens = x_all.shape[0]
    half = tokens // 2
    net = Sends(send_sem, recv_sem)
    pending = []

    def send(src, dst, slot, device):
        c = net.copy(src, dst, slot, device)
        c.start()
        pending.append(c)

    def arrived(dst, slot):
        net.copy(dst, dst, slot, (z, peer(1))).wait_recv()

    locals_ = [
        pltpu.make_async_copy(x_in, x_all.at[:, cols(t)], local_sem.at[0]),
        pltpu.make_async_copy(dy_in, dy_all.at[:, cols(t)], local_sem.at[1]),
        pltpu.make_async_copy(g_in, gain_all.at[:, cols(t)], local_sem.at[2]),
        pltpu.make_async_copy(w1_in.at[:, cols(t)], w1_all.at[cols(t), cols(z)], local_sem.at[3]),
        pltpu.make_async_copy(w3_in.at[:, cols(t)], w3_all.at[cols(t), cols(z)], local_sem.at[4]),
        pltpu.make_async_copy(w2_in.at[cols(t), :], w2_all.at[cols(z), cols(t)], local_sem.at[5]),
    ]
    for c in locals_:
        c.start()

    w_slots = {}
    for s in (6, 7, 2, 3, 4, 5, 1):
        p = peer(s)
        w_slots[s] = [net.slot() for _ in range(4)]
        a, b, c, d = w_slots[s]
        send(w1_in.at[:, cols(p)], w1_all.at[cols(t), cols(z)], a, (z, p))
        send(w3_in.at[:, cols(p)], w3_all.at[cols(t), cols(z)], b, (z, p))
        send(w2_in.at[cols(p), :], w2_all.at[cols(z), cols(t)], c, (z, p))
        send(g_in, gain_all.at[:, cols(t)], d, (z, p))

    lo, hi = pl.ds(0, half), pl.ds(half, half)
    px, py, pd, pc = peer(2), peer(4), peer(6), peer(1)

    def plane_first(src, full, sl):
        send(src.at[lo], full.at[lo, cols(t)], sl[0], (z, px))
        send(src.at[hi], full.at[hi, cols(t)], sl[2], (z, py))
        send(src.at[hi], full.at[hi, cols(t)], sl[1], (z, px))
        send(src.at[lo], full.at[lo, cols(t)], sl[3], (z, py))
        send(src, full.at[:, cols(t)], sl[4], (z, pc))

    def plane_forward(full, sl):
        arrived(full.at[lo, cols(px)], sl[0])
        send(full.at[lo, cols(px)], full.at[lo, cols(px)], sl[5], (z, py))
        send(full.at[lo, cols(px)], full.at[lo, cols(px)], sl[7], (z, pc))
        arrived(full.at[hi, cols(py)], sl[2])
        send(full.at[hi, cols(py)], full.at[hi, cols(py)], sl[6], (z, px))
        send(full.at[hi, cols(py)], full.at[hi, cols(py)], sl[9], (z, pc))

    def plane_rest(full, sl):
        arrived(full.at[hi, cols(px)], sl[1])
        send(full.at[hi, cols(px)], full.at[hi, cols(px)], sl[8], (z, pc))
        arrived(full.at[lo, cols(py)], sl[3])
        send(full.at[lo, cols(py)], full.at[lo, cols(py)], sl[10], (z, pc))
        arrived(full.at[lo, cols(pd)], sl[5])
        send(full.at[lo, cols(pd)], full.at[lo, cols(pd)], sl[11], (z, pc))
        arrived(full.at[hi, cols(pd)], sl[6])
        send(full.at[hi, cols(pd)], full.at[hi, cols(pd)], sl[12], (z, pc))

    def plane_last(full, sl):
        arrived(full.at[:, cols(pc)], sl[4])
        arrived(full.at[lo, cols(peer(3))], sl[7])
        arrived(full.at[hi, cols(peer(3))], sl[8])
        arrived(full.at[hi, cols(peer(5))], sl[9])
        arrived(full.at[lo, cols(peer(5))], sl[10])
        arrived(full.at[lo, cols(peer(7))], sl[11])
        arrived(full.at[hi, cols(peer(7))], sl[12])

    sx = [net.slot() for _ in range(13)]
    sd = [net.slot() for _ in range(13)]
    plane_first(x_in, x_all, sx)

    for c in locals_[2:]:
        c.wait()
    for s in (6, 7, 2, 3, 4, 5, 1):
        p = peer(s)
        a, b, c, d = w_slots[s]
        arrived(w1_all.at[cols(p), cols(z)], a)
        arrived(w3_all.at[cols(p), cols(z)], b)
        arrived(w2_all.at[cols(z), cols(p)], c)
        arrived(gain_all.at[:, cols(p)], d)

    n_z = 4
    up = [[net.slot() for _ in range(3)] for _ in range(n_z)]
    down = [[net.slot() for _ in range(3)] for _ in range(n_z)]

    def chunk(k):
        return (w1_all.at[:, pl.ds(k * LANE, LANE)], w3_all.at[:, pl.ds(k * LANE, LANE)],
                w2_all.at[pl.ds(k * LANE, LANE), :])

    def pass_on(here, k, upward):
        slots = (up if upward else down)[k]
        nxt = here + 1 if upward else here - 1

        @pl.when(z == here)
        def _():
            for ref, slot in zip(chunk(k), slots):
                net.copy(ref, ref, slot, (nxt, t)).start()

    def take(here, k):
        @pl.when(z == here)
        def _():
            for ref, slot in zip(chunk(k), (up if k < here else down)[k]):
                net.copy(ref, ref, slot, (here, pc)).wait_recv()

    for here in range(n_z):
        if here + 1 < n_z:
            pass_on(here, here, True)
        if here > 0:
            pass_on(here, here, False)

    plane_forward(x_all, sx)
    plane_first(dy_in, dy_all, sd)
    plane_rest(x_all, sx)
    locals_[0].wait()
    plane_last(x_all, sx)

    def norm_tile(i, _):
        rows = pl.ds(i * 256, 256)
        xf = x_all[rows, :].astype(F32)
        d = xf.shape[1]
        mu = jnp.sum(xf, axis=1, keepdims=True) / d
        sq = jnp.sum(xf * xf, axis=1, keepdims=True) / d
        r = lax.rsqrt(sq - mu * mu + LN_EPS)
        h_out[rows, :] = (gain_all[0:1, :] * ((xf - mu) * r)).astype(BF16)
        return 0

    for here in range(n_z):
        for k in (here - 1, here + 1):
            if 0 <= k < n_z:
                take(here, k)
                nxt = 2 * here - k
                if 0 <= nxt < n_z:
                    pass_on(here, k, nxt > here)

    lax.fori_loop(0, tokens // 256, norm_tile, 0)
    own_rows = tokens // 8
    x_rows[...] = x_all[pl.ds(pl.multiple_of(t * own_rows, own_rows), own_rows), :]
    plane_forward(dy_all, sd)
    plane_rest(dy_all, sd)
    for dist in (2, 3):
        for here in range(n_z):
            for k in (here - dist, here + dist):
                if 0 <= k < n_z:
                    take(here, k)
                    nxt = here + (1 if k < here else -1)
                    if 0 <= nxt < n_z:
                        pass_on(here, k, nxt > here)
    locals_[1].wait()
    plane_last(dy_all, sd)
    for c in pending:
        c.wait_send()
    for here in range(n_z):
        for upward in (True, False):
            nxt = here + 1 if upward else here - 1
            if 0 <= nxt < n_z:
                for k in (range(here + 1) if upward else range(here, n_z)):
                    @pl.when(z == here)
                    def _(k=k, upward=upward, nxt=nxt):
                        for ref, slot in zip(chunk(k), (up if upward else down)[k]):
                            net.copy(ref, ref, slot, (nxt, t)).wait_send()


N_GATHER = 28 + 26 + 24


def reduce_kernel(m_in, dh_in, w1_in, w3_in, w2_in, x_rows, dy_rows, gain_all,
                  y_out, dx_out, dw1_out, dw3_out, dw2_out, dg_out,
                  m0, m1, m2, e0, e1, e2, out1, out3, out2, in1, in3, in2,
                  y_rows, dx_rows, dg_rows, dg_plane, dg_line,
                  send_sem, recv_sem, local_sem):
    z, t, peer = place()
    net = Sends(send_sem, recv_sem)
    rows = m0.shape[1]
    hr = rows // 2
    px, py, pd, pc = peer(2), peer(4), peer(6), peer(1)
    pending = []
    local_pending = []

    def send(src, dst, slot, device):
        c = net.copy(src, dst, slot, device)
        c.start()
        pending.append(c)

    def arrived(dst, slot):
        net.copy(dst, dst, slot, (z, pc)).wait_recv()

    def block(p):
        return pl.ds(pl.multiple_of(p * rows, rows), rows)

    is_end = jnp.logical_or(z == 0, z == 3)
    is_mid = jnp.logical_or(z == 1, z == 2)
    low = lax.div(3 - z, 2)
    c_end = 3 - 3 * low
    c_mid = 2 - low
    c_mid2 = 3 - c_mid
    c_end2 = 3 - c_end
    inner = z + 2 * low - 1
    outer = z - 2 * low + 1

    mine = ((w1_in, 0), (w3_in, 0), (w2_in, 1))

    def own(p, k):
        ref, axis = mine[p]
        return ref.at[:, cols(k)] if axis == 0 else ref.at[cols(k), :]

    outs = (out1, out3, out2)
    ins = (in1, in3, in2)
    out_slots = [[net.slot() for _ in range(3)] for _ in range(3)]
    in_slots = [[net.slot() for _ in range(3)] for _ in range(2)]
    end_slots = [net.slot() for _ in range(3)]

    @pl.when(is_end)
    def _():
        for q, k in enumerate((c_mid2, c_end2, c_mid)):
            for p in range(3):
                net.copy(own(p, k), outs[p].at[q], out_slots[q][p], (inner, t)).start()

    fin_slots = {s: [net.slot() for _ in range(3)] for s in range(1, 8)}

    def finish_piece(p, src):
        for s in (6, 7, 2, 3, 4, 5, 1):
            q = peer(s)
            if p < 2:
                c = net.copy(src.at[cols(q), :], (dw1_out, dw3_out)[p].at[:, cols(t)], fin_slots[s][p], (z, q))
            else:
                c = net.copy(src.at[:, cols(q)], dw2_out.at[cols(t), :], fin_slots[s][p], (z, q))
            c.start()
        if p < 2:
            pltpu.make_async_copy(src.at[cols(t), :], (dw1_out, dw3_out)[p].at[:, cols(t)], local_sem.at[p]).start()
        else:
            pltpu.make_async_copy(src.at[:, cols(t)], dw2_out.at[cols(t), :], local_sem.at[p]).start()

    def from_outer(q, p, k):
        @pl.when(is_mid)
        def _():
            dst = outs[p].at[q]
            arrived(dst, out_slots[q][p])
            dst[...] += own(p, k)[...]
            net.copy(dst, ins[p].at[q], in_slots[q][p], (inner, t)).start()

    def to_end(p):
        @pl.when(is_mid)
        def _():
            dst = ins[p].at[1]
            arrived(dst, in_slots[1][p])
            dst[...] += own(p, c_end)[...]
            net.copy(dst, dst, end_slots[p], (outer, t)).start()

    def last_mid(p):
        @pl.when(is_mid)
        def _():
            a, b = outs[p].at[2], ins[p].at[0]
            arrived(b, in_slots[0][p])
            arrived(a, out_slots[2][p])
            a[...] += b[...] + own(p, c_mid)[...]
            finish_piece(p, a)

    def last_end(p):
        @pl.when(is_end)
        def _():
            a = ins[p].at[1]
            arrived(a, end_slots[p])
            a[...] += own(p, c_end)[...]
            finish_piece(p, a)

    keep = (t, px, py, pd)
    away = (pc, peer(3), peer(5), peer(7))

    def stage0_start(src, r0, sl):
        for j in (3, 1, 2, 0):
            send(src.at[block(away[j]), :], r0.at[j], sl[j], (z, pc))

    def stage1(src, r0, r1, sl):
        for j in (3, 1, 2, 0):
            arrived(r0.at[j], sl[j])
            r0[j] += src[block(keep[j]), :]
            if j == 3:
                send(r0.at[3, pl.ds(0, hr)], r1.at[0], sl[4], (z, px))
                send(r0.at[3, pl.ds(hr, hr)], r1.at[1], sl[5], (z, py))
            if j == 1:
                send(r0.at[1, pl.ds(0, hr)], r1.at[2], sl[6], (z, px))
            if j == 2:
                send(r0.at[2, pl.ds(hr, hr)], r1.at[3], sl[7], (z, py))

    def stage2(r0, r1, r2, sl):
        arrived(r1.at[0], sl[4])
        r0[2, 0:hr] += r1[0]
        send(r0.at[2, pl.ds(0, hr)], r2.at[0], sl[8], (z, py))
        arrived(r1.at[1], sl[5])
        r0[1, hr:rows] += r1[1]
        send(r0.at[1, pl.ds(hr, hr)], r2.at[1], sl[9], (z, px))

    def stage3(r0, r1, sl):
        arrived(r1.at[2], sl[6])
        r0[0, 0:hr] += r1[2]
        arrived(r1.at[3], sl[7])
        r0[0, hr:rows] += r1[3]

    def stage4(r0, r2, sl):
        arrived(r2.at[0], sl[8])
        r0[0, 0:hr] += r2[0]
        arrived(r2.at[1], sl[9])
        r0[0, hr:rows] += r2[1]

    sm = [net.slot() for _ in range(10)]
    se = [net.slot() for _ in range(10)]
    sy = {s: net.slot() for s in range(1, 8)}
    sdx = {s: net.slot() for s in range(1, 8)}
    sg = {s: net.slot() for s in range(1, 8)}
    sz = {s: net.slot() for s in range(1, 4)}

    def spread(src, dst, slots, local):
        for s in (6, 7, 2, 3, 4, 5, 1):
            q = peer(s)
            send(src.at[:, cols(q)], dst.at[block(t), :], slots[s], (z, q))
        c = pltpu.make_async_copy(src.at[:, cols(t)], dst.at[block(t), :], local_sem.at[local])
        c.start()
        local_pending.append(c)

    stage0_start(m_in, m0, sm)
    stage0_start(dh_in, e0, se)
    stage1(m_in, m0, m1, sm)
    from_outer(0, 0, c_mid2)
    stage2(m0, m1, m2, sm)
    stage1(dh_in, e0, e1, se)
    from_outer(0, 1, c_mid2)
    stage3(m0, m1, sm)
    from_outer(0, 2, c_mid2)
    stage4(m0, m2, sm)
    y_rows[...] = (x_rows[...].astype(F32) + m0[0]).astype(BF16)
    spread(y_rows, y_out, sy, 3)
    from_outer(1, 0, c_end2)
    stage2(e0, e1, e2, se)
    from_outer(1, 1, c_end2)
    to_end(0)
    stage3(e0, e1, se)
    from_outer(1, 2, c_end2)
    to_end(1)
    stage4(e0, e2, se)

    xf = x_rows[...].astype(F32)
    d = xf.shape[1]
    mu = jnp.sum(xf, axis=1, keepdims=True) / d
    sq = jnp.sum(xf * xf, axis=1, keepdims=True) / d
    r = lax.rsqrt(sq - mu * mu + LN_EPS)
    xhat = (xf - mu) * r
    dh = e0[0]
    e = dh * gain_all[0:1, :]
    e_mean = jnp.sum(e, axis=1, keepdims=True) / d
    ex_mean = jnp.sum(e * xhat, axis=1, keepdims=True) / d
    dx_rows[...] = (dy_rows[...].astype(F32) + r * (e - e_mean - xhat * ex_mean)).astype(BF16)
    dg_rows[...] = jnp.sum((dh * xhat).reshape(rows // 8, 8, d), axis=0)
    spread(dx_rows, dx_out, sdx, 4)
    for s in range(1, 8):
        q = peer(s)
        send(dg_rows.at[:, cols(q)], dg_plane.at[s - 1], sg[s], (z, q))
    to_end(2)
    last_end(0)
    total = dg_rows[:, cols(t)]
    for s in range(1, 8):
        arrived(dg_plane.at[s - 1], sg[s])
        total = total + dg_plane[s - 1]
    dg_line[0] = total
    for s in range(1, 4):
        send(dg_line.at[0], dg_line.at[s], sz[s], (lax.rem(z + s, 4), t))
    last_end(1)
    last_end(2)
    last_mid(0)
    for s in range(1, 4):
        arrived(dg_line.at[s], sz[s])
    ordered = [dg_line[lax.rem(z - s + 4, 4)] for s in range(4)]
    dg_out[...] = (ordered[0] + ordered[1]) + (ordered[2] + ordered[3])
    last_mid(1)
    last_mid(2)

    for s in range(1, 8):
        q = peer(s)
        arrived(y_out.at[block(q), :], sy[s])
        arrived(dx_out.at[block(q), :], sdx[s])
        arrived(dw1_out.at[:, cols(q)], fin_slots[s][0])
        arrived(dw3_out.at[:, cols(q)], fin_slots[s][1])
        arrived(dw2_out.at[cols(q), :], fin_slots[s][2])
    for c in pending:
        c.wait_send()
    for c in local_pending:
        c.wait()
    for p in range(3):
        if p < 2:
            pltpu.make_async_copy(outs[p].at[2, cols(t), :], (dw1_out, dw3_out)[p].at[:, cols(t)], local_sem.at[p]).wait()
        else:
            pltpu.make_async_copy(outs[p].at[2, :, cols(t)], dw2_out.at[cols(t), :], local_sem.at[p]).wait()
        for s in range(1, 8):
            if p < 2:
                net.copy(outs[p].at[2, cols(t), :], (dw1_out, dw3_out)[p].at[:, cols(t)], fin_slots[s][p], (z, pc)).wait_send()
            else:
                net.copy(outs[p].at[2, :, cols(t)], dw2_out.at[cols(t), :], fin_slots[s][p], (z, pc)).wait_send()

    @pl.when(is_end)
    def _():
        for q, k in enumerate((c_mid2, c_end2, c_mid)):
            for p in range(3):
                net.copy(own(p, k), outs[p].at[q], out_slots[q][p], (inner, t)).wait_send()

    @pl.when(is_mid)
    def _():
        for p in range(3):
            for q in range(2):
                net.copy(outs[p].at[q], ins[p].at[q], in_slots[q][p], (inner, t)).wait_send()
            net.copy(ins[p].at[1], ins[p].at[1], end_slots[p], (outer, t)).wait_send()


N_REDUCE = 9 + 9 + 21 + 20 + 21 + 3


def contract_rows(a, b):
    return lax.dot_general(a, b, (((0,), (0,)), ((), ())), preferred_element_type=F32)


def contract_cols(a, b):
    return lax.dot_general(a, b, (((1,), (1,)), ((), ())), preferred_element_type=F32)


def solution(mesh):
    n_t = mesh.shape["tx"]
    n_z = mesh.shape["ty"]

    def local_step(x_blk, dy_blk, gain_blk, w1_blk, w3_blk, w2_blk):
        tokens, lane = x_blk.shape
        d = lane * n_t
        f = w1_blk.shape[1] // n_t * n_z
        rows = tokens // n_t
        gain8 = jnp.broadcast_to(gain_blk[None, :], (8, lane))
        any_spec = pl.BlockSpec(memory_space=pl.ANY)
        vmem = pl.BlockSpec(memory_space=pltpu.VMEM)
        s = jax.ShapeDtypeStruct
        h, dy_all, x_rows, gain_all, w1, w3, w2 = pl.pallas_call(
            gather_kernel,
            out_shape=(s((tokens, d), BF16), s((tokens, d), BF16), s((rows, d), BF16), s((8, d), F32),
                       s((d, f), BF16), s((d, f), BF16), s((f, d), BF16)),
            in_specs=[any_spec] * 6,
            out_specs=[vmem] * 7,
            scratch_shapes=[pltpu.VMEM((tokens, d), BF16), pltpu.SemaphoreType.DMA((N_GATHER,)),
                            pltpu.SemaphoreType.DMA((N_GATHER,)), pltpu.SemaphoreType.DMA((6,))],
            compiler_params=pltpu.CompilerParams(has_side_effects=True, vmem_limit_bytes=48 * 2**20),
            name="gather",
        )(x_blk, dy_blk, gain8, w1_blk, w3_blk, w2_blk)

        u = jnp.dot(h, w1, preferred_element_type=F32)
        v = jnp.dot(h, w3, preferred_element_type=F32)
        sig = jax.nn.sigmoid(u)
        swish = u * sig
        act = (swish * v).astype(BF16)
        da = contract_cols(dy_all, w2)
        du = (da * v * sig * (1.0 + u * (1.0 - sig))).astype(BF16)
        dv = (da * swish).astype(BF16)
        dw2 = contract_rows(act, dy_all)
        dw1 = contract_rows(h, du)
        dw3 = contract_rows(h, dv)
        m = jnp.dot(act, w2, preferred_element_type=F32)
        dh = contract_cols(du, w1) + contract_cols(dv, w3)
        dy_rows = lax.dynamic_slice(dy_all, (lax.axis_index("tx") * rows, 0), (rows, d))

        y, dx, dw1_o, dw3_o, dw2_o, dg = pl.pallas_call(
            reduce_kernel,
            out_shape=(s((tokens, lane), BF16), s((tokens, lane), BF16), s((lane, w1_blk.shape[1]), F32),
                       s((lane, w1_blk.shape[1]), F32), s((w1_blk.shape[1], lane), F32), s((8, lane), F32)),
            in_specs=[vmem] * 8,
            out_specs=[any_spec] * 5 + [vmem],
            scratch_shapes=[
                pltpu.VMEM((4, rows, d), F32), pltpu.VMEM((4, rows // 2, d), F32), pltpu.VMEM((2, rows // 2, d), F32),
                pltpu.VMEM((4, rows, d), F32), pltpu.VMEM((4, rows // 2, d), F32), pltpu.VMEM((2, rows // 2, d), F32),
                pltpu.VMEM((3, d, lane), F32), pltpu.VMEM((3, d, lane), F32), pltpu.VMEM((3, lane, d), F32),
                pltpu.VMEM((2, d, lane), F32), pltpu.VMEM((2, d, lane), F32), pltpu.VMEM((2, lane, d), F32),
                pltpu.VMEM((rows, d), BF16), pltpu.VMEM((rows, d), BF16), pltpu.VMEM((8, d), F32),
                pltpu.VMEM((7, 8, lane), F32), pltpu.VMEM((4, 8, lane), F32),
                pltpu.SemaphoreType.DMA((N_REDUCE,)), pltpu.SemaphoreType.DMA((N_REDUCE,)),
                pltpu.SemaphoreType.DMA((5,))],
            compiler_params=pltpu.CompilerParams(has_side_effects=True, vmem_limit_bytes=62 * 2**20),
            name="reduce",
        )(m, dh, dw1, dw3, dw2, x_rows, dy_rows, gain_all)
        return y, dx, dw1_o, dw3_o, dw2_o, jnp.sum(dg, axis=0)

    return jax.shard_map(
        local_step, mesh=mesh,
        in_specs=(P("ty", "tx"), P("ty", "tx"), P("tx"), P("tx", "ty"), P("tx", "ty"), P("ty", "tx")),
        out_specs=(P("ty", "tx"), P("ty", "tx"), P("tx", "ty"), P("tx", "ty"), P("ty", "tx"), P("tx")),
        check_vma=False)
```

time: 1200 us -> 266 us (0.22)
  the two profiles are of different devices: /device:TPU:0 before, /device:TPU:11 now
where the time goes in v1:
time: 266 us; the launch traced here: 265 us
  Pallas kernels  210 us (79%)
  matrix products  36.8 us (14%)
  local copies, waits for them, and re-layouts  16 us (6%)
    pallas_call x1, Pallas kernels, local_step(): pl.pallas_call(reduce_kernel, out_shape=(s((tokens, lane), BF16), s((toke...  134 us
    pallas_call x1, Pallas kernels, local_step(): pl.pallas_call(gather_kernel, out_shape=(s((tokens, d), BF16), s((tokens,...  76.3 us
    unnamed x25, local copies, waits for them, and re-layouts  13.3 us
    dot_general x3, matrix products, contract_cols(): lax.dot_general(a, b, (((1,), (1,)), ((), ())), preferred_element_type=F32)  13 us
    dot_general x3, matrix products, contract_rows(): lax.dot_general(a, b, (((0,), (0,)), ((), ())), preferred_element_type=F32)  11.1 us
    dot_general x1, matrix products, local_step(): m = jnp.dot(act, w2, preferred_element_type=F32)  5.68 us

profile of v1, /device:TPU:11, one launch (start us, length us, event | category | flops | bytes accessed | tf_op | source)
XLA Modules:
  0.0 265.2 jit_solution(4841908931916714846)
XLA Ops:
  0.6 0.7 broadcast_in_dim.2.g_in
  1.3 1.0 copy-done
  2.3 1.0 copy-done.1
  3.4 0.9 copy-done.3
  4.3 0.9 copy-done.4
  5.3 0.9 copy-done.5
  6.2 76.3 %gather.1 = (bf16[2048,1024]{1,0:T(8,128)(2,1)}, bf16[2048,1024]{1,0:T(8,128)(2,1)}, bf16[256,1024]{1,0:T(8,128)(2,1)S(1)}, f32[8,1024]{1,0:T(8,128)S(1)}, bf16[...) custom-call(bf16[2048,128]{1,0:T(8,128)(2,1)S(1)} %copy-done, ...), custom_call_target="tpu_custom_call" | custom-call | tf_op jit(solution)/shard_map/gather/pallas_call | solution.py:495
  82.5 0.0 copy-start.2
  82.6 0.0 copy-start.6
  82.6 2.1 constant_dynamic-slice_fusion.dy_rows
  84.6 4.7 %fusion.1 = f32[2048,512]{1,0:T(8,128)S(1)} fusion(bf16[2048,1024]{1,0:T(8,128)(2,1)} %get-tuple-element.19, bf16[1024,512]{1,0:T(8,128)(2,1)S(1)} %get-tuple-element.20), kind=kOutput, calls=%fused_computation.7 | convolution fusion | flops 2147483648 | bytes 9437184 | tf_op jit(solution)/shard_map/dot_general | solution.py:507
  89.4 0.0 copy-done.2
  89.4 0.0 copy-done.6
  89.4 0.0 copy-done.7
  89.4 0.0 copy-start.9
  89.4 2.3 fusion.2
  91.8 0.0 copy-done.9
  91.8 4.6 %multiply_convert_fusion = (bf16[2048,512]{1,0:T(8,128)(2,1)S(1)}, bf16[2048,512]{1,0:T(8,128)(2,1)S(1)}, bf16[2048,512]{1,0:T(8,128)(2,1)S(1)}) fusion(f32[2048,512]{1,0:T(8,128)S(1)} %fusion.1, f32[2048,512]{1,0:T(8,128)S(1)} %fusion.2, bf16[2048,1024]{1,0:T(8,128)(2,1)S(1)} %copy-done.9, bf16[512,1024]{1,0:T(8,128)(2,1)S(1)} %get-tuple-element.22), kind=kOutput, calls=%fused_computation | convolution fusion | flops 2163212288 | bytes 19922944 | tf_op jit(solution)/shard_map/dot_general | solution.py:479
  96.4 3.7 %fusion.7.w2_in = f32[512,1024]{1,0:T(8,128)} fusion(bf16[2048,512]{1,0:T(8,128)(2,1)S(1)} %get-tuple-element.34, bf16[2048,1024]{1,0:T(8,128)(2,1)S(1)} %copy-done.9), kind=kOutput, calls=%fused_computation.13 | convolution fusion | flops 2147483648 | bytes 8388608 | tf_op jit(solution)/shard_map/dot_general | solution.py:475
  100.1 3.7 %fusion.6.w3_in = f32[1024,512]{1,0:T(8,128)} fusion(bf16[2048,1024]{1,0:T(8,128)(2,1)S(1)} %copy-done.7, bf16[2048,512]{1,0:T(8,128)(2,1)S(1)} %get-tuple-element.32), kind=kOutput, calls=%fused_computation.12 | convolution fusion | flops 2147483648 | bytes 8388608 | tf_op jit(solution)/shard_map/dot_general | solution.py:475
  103.8 3.7 %fusion.5.w1_in = f32[1024,512]{1,0:T(8,128)} fusion(bf16[2048,1024]{1,0:T(8,128)(2,1)S(1)} %copy-done.7, bf16[2048,512]{1,0:T(8,128)(2,1)S(1)} %get-tuple-element.33), kind=kOutput, calls=%fused_computation.11 | convolution fusion | flops 2147483648 | bytes 8388608 | tf_op jit(solution)/shard_map/dot_general | solution.py:475
  107.5 2.5 fusion.4
  109.9 5.9 %convolution_add_fusion.dh_in = f32[2048,1024]{1,0:T(8,128)} fusion(f32[2048,1024]{1,0:T(8,128)S(1)} %fusion.4, bf16[2048,512]{1,0:T(8,128)(2,1)S(1)} %get-tuple-element.32, bf16[1024,512]{1,0:T(8,128)(2,1)S(1)} %get-tuple-element.21), kind=kOutput, calls=%fused_computation.5 | convolution fusion | flops 2149580800 | bytes 19922944 | tf_op jit(solution)/shard_map/dot_general | solution.py:479
  115.9 5.7 %fusion.3.m_in = f32[2048,1024]{1,0:T(8,128)} fusion(bf16[2048,512]{1,0:T(8,128)(2,1)S(1)} %get-tuple-element.34, bf16[512,1024]{1,0:T(8,128)(2,1)S(1)} %get-tuple-element.22), kind=kOutput, calls=%fused_computation.9 | convolution fusion | flops 2147483648 | bytes 11534336 | tf_op jit(solution)/shard_map/dot_general | solution.py:518
  121.6 134.1 %reduce.1 = (bf16[2048,128]{1,0:T(8,128)(2,1)}, bf16[2048,128]{1,0:T(8,128)(2,1)}, f32[128,1024]{1,0:T(8,128)}, f32[128,1024]{1,0:T(8,128)}, f32[1024,128]{1,0:T(8,128)}, /*index=5*/f32[8,128]{1,0:T(8,128)}) custom-call(f32[2048,1024]{1,0:T(8,128)} %fusion.3.m_in, f32[2048,1024]{1,0:T(8,128)} %convolution_add_fusion.dh_in, f32[1024,512]{1,0:T(8,128)} %fusion.5.w1_in, ...), custom_call_target="tpu_custom_call" | custom-call | tf_op jit(solution)/shard_map/reduce/pallas_call | solution.py:522
  255.7 0.0 copy-start.8
  255.7 1.3 reduce_sum.9
  256.9 1.9 copy.17
  258.8 1.9 copy.18
  260.7 1.9 copy.19
  262.6 1.9 copy.20
  264.5 0.8 copy.21
  (7 shorter events, 0.0 us)
Async XLA Ops:
  1.3 1.0 copy-start
  2.3 1.0 copy-start.1
  3.4 0.9 copy-start.3
  4.3 0.9 copy-start.4
  5.3 0.9 copy-start.5
  82.5 6.8 %copy-start.2 = (bf16[256,1024]{1,0:T(8,128)(2,1)}, bf16[256,1024]{1,0:T(8,128)(2,1)S(1)}, u32[]{:S(2)}) copy-start(bf16[256,1024]{1,0:T(8,128)(2,1)S(1)} %get-tuple-element.24.x_rows) | copy-start | bytes 1572868
  82.6 6.8 %copy-start.6 = (f32[8,1024]{1,0:T(8,128)}, f32[8,1024]{1,0:T(8,128)S(1)}, u32[]{:S(2)}) copy-start(f32[8,1024]{1,0:T(8,128)S(1)} %get-tuple-element.25.gain_all) | copy-start | bytes 98308
  84.6 4.8 %copy-start.7 = (bf16[2048,1024]{1,0:T(8,128)(2,1)S(1)}, bf16[2048,1024]{1,0:T(8,128)(2,1)}, u32[]{:S(2)}) copy-start(bf16[2048,1024]{1,0:T(8,128)(2,1)} %get-tuple-element.19) | copy-start | bytes 12582916
  89.4 2.4 copy-start.9
  255.7 8.8 %copy-start.8 = (f32[1024,128]{1,0:T(8,128)S(1)}, f32[1024,128]{1,0:T(8,128)}, u32[]{:S(2)}) copy-start(f32[1024,128]{1,0:T(8,128)} %get-tuple-element.45) | copy-start | bytes 1572868

commit v2 on v0

v2 whole, which is shorter than its diff:
```python
import jax
import jax.numpy as jnp
from jax import lax
from jax.experimental import pallas as pl
from jax.experimental.pallas import tpu as pltpu
from jax.sharding import PartitionSpec as P

LN_EPS = 1e-6
F32 = jnp.float32
BF16 = jnp.bfloat16
MESH = pl.DeviceIdType.MESH
LANE = 128
N_T = 8
N_Z = 4
PIECES = 6
ROWS = 384 // PIECES


def cols(k, width=LANE):
    return pl.ds(pl.multiple_of(k * width, width), width)


def dot(a, b):
    return jnp.dot(a, b, preferred_element_type=F32)


def dot_cols(a, b):
    return lax.dot_general(a, b, (((1,), (1,)), ((), ())), preferred_element_type=F32)


N_PLANE = 28 + 26
N_RED = 20 + 21 + 3
N_SUM = 6 * PIECES


def step_kernel(x_in, dy_in, g_in, w1_in, w3_in, w2_in,
                y_out, dx_out, dw_out, dg_out,
                x_all, h_all, dy_all, gain_all, w13, w2, act, act_t, duv_t, dw,
                m_away, m0, m1, m2, e_away, e0, e1, e2, outs, ins,
                x_rows, y_rows, dx_rows, dg_rows, dg_plane, dg_line,
                send_sem, recv_sem, wz_send, wz_recv, sum_send, sum_recv, fin_send, fin_recv,
                red_send, red_recv, local_sem):
    z = lax.axis_index("ty")
    t = lax.axis_index("tx")
    core = lax.rem(t, 2)
    xbit = lax.rem(lax.div(t, 2), 2)
    ybit = lax.div(t, 4)
    flips = (1 - 2 * core, 2 - 4 * xbit, 4 - 8 * ybit)
    duv = x_all

    def peer(s):
        out = t
        for bit in range(3):
            if s >> bit & 1:
                out = out + flips[bit]
        return out

    px, py, pd, pc = peer(2), peer(4), peer(6), peer(1)
    order = (2, 4, 3, 5, 6, 7, 1)
    tokens = x_all.shape[0]
    half = tokens // 2
    rows = tokens // N_T
    hr = rows // 2

    low = lax.div(3 - z, 2)
    is_end = jnp.logical_or(z == 0, z == 3)
    is_mid = jnp.logical_or(z == 1, z == 2)
    c_end = 3 - 3 * low
    c_mid = 2 - low
    c_mid2 = 3 - c_mid
    c_end2 = 3 - c_end
    inner = z + 2 * low - 1
    outer = z - 2 * low + 1

    def rcopy(src, dst, ssem, rsem, device):
        return pltpu.make_async_remote_copy(src_ref=src, dst_ref=dst, send_sem=ssem, recv_sem=rsem,
                                            device_id=device, device_id_type=MESH)

    count = [0]

    def slot():
        count[0] += 1
        return count[0] - 1

    pending = []

    def send(src, dst, sl, device):
        c = rcopy(src, dst, send_sem.at[sl], recv_sem.at[sl], device)
        c.start()
        pending.append(c)
        return c

    def arrived(dst, sl):
        rcopy(dst, dst, send_sem.at[sl], recv_sem.at[sl], (z, pc)).wait_recv()

    loc = [
        pltpu.make_async_copy(w1_in.at[:, cols(t)], w13.at[cols(t), cols(2 * z)], local_sem.at[0]),
        pltpu.make_async_copy(w3_in.at[:, cols(t)], w13.at[cols(t), cols(2 * z + 1)], local_sem.at[1]),
        pltpu.make_async_copy(w2_in.at[cols(t), :], w2.at[cols(z), cols(t)], local_sem.at[2]),
        pltpu.make_async_copy(g_in, gain_all.at[:, cols(t)], local_sem.at[3]),
        pltpu.make_async_copy(x_in, x_all.at[:, cols(t)], local_sem.at[4]),
        pltpu.make_async_copy(dy_in, dy_all.at[:, cols(t)], local_sem.at[5]),
    ]
    for c in loc:
        c.start()

    w_slots = {}
    for s in order:
        p = peer(s)
        w_slots[s] = [slot() for _ in range(4)]
        a, b, c, d = w_slots[s]
        send(w1_in.at[:, cols(p)], w13.at[cols(t), cols(2 * z)], a, (z, p))
        send(w3_in.at[:, cols(p)], w13.at[cols(t), cols(2 * z + 1)], b, (z, p))
        send(w2_in.at[cols(p), :], w2.at[cols(z), cols(t)], c, (z, p))
        send(g_in, gain_all.at[:, cols(t)], d, (z, p))

    lo, hi = pl.ds(0, half), pl.ds(half, half)

    def plane_first(src, full, sl):
        return [send(src.at[lo], full.at[lo, cols(t)], sl[0], (z, px)),
                send(src.at[hi], full.at[hi, cols(t)], sl[2], (z, py)),
                send(src.at[hi], full.at[hi, cols(t)], sl[1], (z, px)),
                send(src.at[lo], full.at[lo, cols(t)], sl[3], (z, py)),
                send(src, full.at[:, cols(t)], sl[4], (z, pc))]

    def forward(ref, sl, device):
        return send(ref, ref, sl, (z, device))

    def plane_forward(full, sl):
        a, b = full.at[lo, cols(px)], full.at[hi, cols(py)]
        arrived(a, sl[0])
        out = [forward(a, sl[5], py), forward(a, sl[7], pc)]
        arrived(b, sl[2])
        return out + [forward(b, sl[6], px), forward(b, sl[9], pc)]

    def plane_rest(full, sl):
        out = []
        for rr, p, i, o in ((hi, px, 1, 8), (lo, py, 3, 10), (lo, pd, 5, 11), (hi, pd, 6, 12)):
            ref = full.at[rr, cols(p)]
            arrived(ref, sl[i])
            out.append(forward(ref, sl[o], pc))
        return out

    def plane_last(full, sl):
        arrived(full.at[:, cols(pc)], sl[4])
        for rr, s, i in ((lo, 3, 7), (hi, 3, 8), (hi, 5, 9), (lo, 5, 10), (lo, 7, 11), (hi, 7, 12)):
            arrived(full.at[rr, cols(peer(s))], sl[i])

    sx = [slot() for _ in range(13)]
    sd = [slot() for _ in range(13)]
    x_sends = plane_first(x_in, x_all, sx)

    def wz(k, p, sl, device):
        a, b = w13.at[cols(p), cols(k, 2 * LANE)], w2.at[cols(k), cols(p)]
        return (rcopy(a, a, wz_send.at[sl, p, 0], wz_recv.at[sl, p, 0], (device, t)),
                rcopy(b, b, wz_send.at[sl, p, 1], wz_recv.at[sl, p, 1], (device, t)))

    def wz_own(p):
        @pl.when(is_end)
        def _():
            for c in wz(c_end, p, 3, inner):
                c.start()

        @pl.when(is_mid)
        def _():
            for c in wz(c_mid, p, 0, outer) + wz(c_mid, p, 4, inner):
                c.start()

    for c in loc[:3]:
        c.wait()
    wz_own(t)
    for s in (1, 2, 4, 3, 5, 6, 7):
        p = peer(s)
        a, b, c, d = w_slots[s]
        arrived(w13.at[cols(p), cols(2 * z)], a)
        arrived(w13.at[cols(p), cols(2 * z + 1)], b)
        arrived(w2.at[cols(z), cols(p)], c)
        arrived(gain_all.at[:, cols(p)], d)
        wz_own(p)

    x_sends += plane_forward(x_all, sx)
    plane_first(dy_in, dy_all, sd)

    def each_block(fn):
        lax.fori_loop(0, N_T, lambda p, c: (fn(p), c)[1], 0)

    def wz_wait(k, p, sl):
        for c in wz(k, p, sl, inner):
            c.wait_recv()

    def hop_one(p):
        wz_wait(c_end, p, 3)
        for c in wz(c_end, p, 5, inner):
            c.start()
        wz_wait(c_mid2, p, 4)
        for c in wz(c_mid2, p, 1, outer):
            c.start()

    def hop_two(p):
        wz_wait(c_end2, p, 5)
        for c in wz(c_end2, p, 2, outer):
            c.start()

    @pl.when(is_mid)
    def _():
        each_block(hop_one)

    x_sends += plane_rest(x_all, sx)
    for c in loc[3:5]:
        c.wait()
    plane_last(x_all, sx)

    def norm(xf):
        d = xf.shape[1]
        mu = jnp.sum(xf, axis=1, keepdims=True) / d
        sq = jnp.sum(xf * xf, axis=1, keepdims=True) / d
        r = lax.rsqrt(sq - mu * mu + LN_EPS)
        return (xf - mu) * r, r

    def norm_tile(i, carry):
        rr = pl.ds(pl.multiple_of(i * rows, rows), rows)
        xhat, _ = norm(x_all[rr, :].astype(F32))
        h_all[rr, :] = (gain_all[0:1, :] * xhat).astype(BF16)
        return carry

    def block(p):
        return pl.ds(pl.multiple_of(p * rows, rows), rows)

    lax.fori_loop(0, N_T, norm_tile, 0)
    x_rows[...] = x_all[block(t), :]
    plane_forward(dy_all, sd)

    @pl.when(is_mid)
    def _():
        each_block(hop_two)

    plane_rest(dy_all, sd)
    loc[5].wait()
    plane_last(dy_all, sd)
    for c in x_sends:
        c.wait_send()

    def piece(p):
        return pl.ds(p * ROWS, ROWS)

    def sum_copy(src, dst, sl, p, device):
        return rcopy(src, dst, sum_send.at[sl, p], sum_recv.at[sl, p], (device, t))

    def from_end(q, k, p):
        return sum_copy(dw.at[k, piece(p)], outs.at[q, piece(p)], q, p, inner)

    def end_send(q, k):
        @pl.when(is_end)
        def _():
            for p in range(PIECES):
                from_end(q, k, p).start()

    def chunk_step(i, carry):
        b = i + (1 - 2 * lax.rem(i, 2)) * (1 - lax.div(i, 2))
        k = low * b + (1 - low) * (3 - b)

        for step, sl in ((0, 0), (2, 1), (3, 2)):
            @pl.when(jnp.logical_and(is_end, i == step))
            def _(sl=sl):
                each_block(lambda p: wz_wait(k, p, sl))

        def tile(j, c):
            rr = block(j)
            uv = dot(h_all[rr, :], w13[:, cols(k, 2 * LANE)])
            da = dot_cols(dy_all[rr, :], w2[cols(k), :])
            u, v = uv[:, :LANE], uv[:, LANE:]
            sig = jax.nn.sigmoid(u)
            swish = u * sig
            a = (swish * v).astype(BF16)
            du = (da * v * sig * (1.0 + u * (1.0 - sig))).astype(BF16)
            dv = (da * swish).astype(BF16)
            act[rr, cols(k)] = a
            duv[rr, cols(2 * k)] = du
            duv[rr, cols(2 * k + 1)] = dv
            act_t[:, rr] = a.T
            duv_t[0:LANE, rr] = du.T
            duv_t[LANE:, rr] = dv.T
            return c

        lax.fori_loop(0, N_T, tile, 0)

        def grad(n, c):
            nn = cols(n, 2 * LANE)
            dw[k, 0:2 * LANE, nn] = dot(duv_t[...], h_all[:, nn])
            dw[k, 2 * LANE:, nn] = dot(act_t[...], dy_all[:, nn])
            return c

        lax.fori_loop(0, dy_all.shape[1] // (2 * LANE), grad, 0)

        @pl.when(i == 0)
        def _():
            end_send(2, c_mid)
        return carry

    lax.fori_loop(0, N_Z, chunk_step, 0)
    end_send(1, c_end2)
    end_send(0, c_mid2)

    def stage0(away, r0, make, base):
        def body(j, c):
            fx, fy = 1 - lax.div(j, 2), 1 - lax.rem(j, 2)
            i = fx + 2 * fy
            away[i] = make(block(pc + fx * flips[1] + fy * flips[2]))
            rcopy(away.at[i], r0.at[i], red_send.at[base + i], red_recv.at[base + i], (z, pc)).start()
            return c
        lax.fori_loop(0, 4, body, 0)

    def stage1(r0, make, base):
        def body(j, c):
            fx, fy = 1 - lax.div(j, 2), 1 - lax.rem(j, 2)
            i = fx + 2 * fy
            rcopy(r0.at[i], r0.at[i], red_send.at[base + i], red_recv.at[base + i], (z, pc)).wait_recv()
            r0[i] += make(block(t + fx * flips[1] + fy * flips[2]))
            return c
        lax.fori_loop(0, 4, body, 0)

    def rsend(src, dst, sl, device):
        c = rcopy(src, dst, red_send.at[sl], red_recv.at[sl], device)
        c.start()
        pending.append(c)

    def rarrived(dst, sl):
        rcopy(dst, dst, red_send.at[sl], red_recv.at[sl], (z, pc)).wait_recv()

    a_half, b_half = pl.ds(0, hr), pl.ds(hr, hr)

    def stage1_send(r0, r1, base):
        rsend(r0.at[3, a_half], r1.at[0], base + 4, (z, px))
        rsend(r0.at[3, b_half], r1.at[1], base + 5, (z, py))
        rsend(r0.at[1, a_half], r1.at[2], base + 6, (z, px))
        rsend(r0.at[2, b_half], r1.at[3], base + 7, (z, py))

    def stage2(r0, r1, r2, base):
        rarrived(r1.at[0], base + 4)
        r0[2, 0:hr] += r1[0]
        rsend(r0.at[2, a_half], r2.at[0], base + 8, (z, py))
        rarrived(r1.at[1], base + 5)
        r0[1, hr:rows] += r1[1]
        rsend(r0.at[1, b_half], r2.at[1], base + 9, (z, px))

    def stage3(r0, r1, base):
        rarrived(r1.at[2], base + 6)
        r0[0, 0:hr] += r1[2]
        rarrived(r1.at[3], base + 7)
        r0[0, hr:rows] += r1[3]

    def stage4(r0, r2, base):
        rarrived(r2.at[0], base + 8)
        r0[0, 0:hr] += r2[0]
        rarrived(r2.at[1], base + 9)
        r0[0, hr:rows] += r2[1]

    def make_m(rr):
        return dot(act[rr, :], w2[...])

    def make_dh(rr):
        return dot_cols(duv[rr, :], w13[...])

    stage0(m_away, m0, make_m, 0)
    stage0(e_away, e0, make_dh, 10)
    stage1(m0, make_m, 0)
    stage1_send(m0, m1, 0)
    stage1(e0, make_dh, 10)
    stage1_send(e0, e1, 10)

    def finish(src, p):
        for s in (6, 7, 2, 4, 3, 5, 1):
            q = peer(s)
            rcopy(src.at[:, cols(q)], dw_out.at[t, piece(p)], fin_send.at[s, p], fin_recv.at[s, p], (z, q)).start()
        pltpu.make_async_copy(src.at[:, cols(t)], dw_out.at[t, piece(p)], fin_send.at[0, p]).start()

    def pass_in(q, k, p):
        @pl.when(is_mid)
        def _():
            ref = outs.at[q, piece(p)]
            sum_copy(ref, ref, q, p, outer).wait_recv()
            outs[q, p * ROWS:(p + 1) * ROWS] += dw[k, p * ROWS:(p + 1) * ROWS]
            sum_copy(ref, ins.at[q, piece(p)], 3 + q, p, inner).start()

    def pass_out(p):
        @pl.when(is_mid)
        def _():
            ref = ins.at[1, piece(p)]
            sum_copy(ref, ref, 4, p, inner).wait_recv()
            ins[1, p * ROWS:(p + 1) * ROWS] += dw[c_end, p * ROWS:(p + 1) * ROWS]
            sum_copy(ref, ref, 5, p, outer).start()

    def last_mid(p):
        @pl.when(is_mid)
        def _():
            a, b = outs.at[2, piece(p)], ins.at[0, piece(p)]
            sum_copy(b, b, 3, p, inner).wait_recv()
            sum_copy(a, a, 2, p, outer).wait_recv()
            rr = slice(p * ROWS, (p + 1) * ROWS)
            outs[2, rr] += ins[0, rr] + dw[c_mid, rr]
            finish(a, p)

    def last_end(p):
        @pl.when(is_end)
        def _():
            a = ins.at[1, piece(p)]
            sum_copy(a, a, 5, p, inner).wait_recv()
            rr = slice(p * ROWS, (p + 1) * ROWS)
            ins[1, rr] += dw[c_end, rr]
            finish(a, p)

    def spread(src, dst, base, local):
        for s in (6, 7, 2, 4, 3, 5, 1):
            q = peer(s)
            rsend(src.at[:, cols(q)], dst.at[block(t), :], base + s - 1, (z, q))
        c = pltpu.make_async_copy(src.at[:, cols(t)], dst.at[block(t), :], local_sem.at[local])
        c.start()
        loc.append(c)

    def make_y():
        stage4(m0, m2, 0)
        y_rows[...] = (x_rows[...].astype(F32) + m0[0]).astype(BF16)
        spread(y_rows, y_out, 20, 6)

    def make_dx():
        stage4(e0, e2, 10)
        xhat, r = norm(x_rows[...].astype(F32))
        d = xhat.shape[1]
        dh = e0[0]
        e = dh * gain_all[0:1, :]
        e_mean = jnp.sum(e, axis=1, keepdims=True) / d
        ex_mean = jnp.sum(e * xhat, axis=1, keepdims=True) / d
        dy_rows = dy_all[block(t), :].astype(F32)
        dx_rows[...] = (dy_rows + r * (e - e_mean - xhat * ex_mean)).astype(BF16)
        dg_rows[...] = jnp.sum((dh * xhat).reshape(rows // 8, 8, d), axis=0)
        spread(dx_rows, dx_out, 27, 7)
        for s in order:
            rsend(dg_rows.at[:, cols(peer(s))], dg_plane.at[s - 1], 34 + s - 1, (z, peer(s)))

    def gain_plane():
        total = dg_rows[:, cols(t)]
        for s in range(1, 8):
            rarrived(dg_plane.at[s - 1], 34 + s - 1)
            total = total + dg_plane[s - 1]
        dg_line[0] = total
        for s in range(1, 4):
            rsend(dg_line.at[0], dg_line.at[s], 40 + s, (lax.rem(z + s, 4), t))

    def gain_line():
        for s in range(1, 4):
            rarrived(dg_line.at[s], 40 + s)
        parts = [dg_line[lax.rem(z - s + 4, 4)] for s in range(4)]
        dg_out[...] = (parts[0] + parts[1]) + (parts[2] + parts[3])

    per = 33.7 / PIECES
    plan = [(90, lambda: stage2(m0, m1, m2, 0)), (101, lambda: stage3(m0, m1, 0)),
            (113, lambda: stage2(e0, e1, e2, 10)), (124, lambda: stage3(e0, e1, 10)),
            (135, make_y), (147, make_dx), (151, gain_plane), (157, gain_line)]
    for p in range(PIECES):
        done = 83 + per * (p + 1)
        plan.append((done, lambda p=p: pass_in(1, c_end2, p)))
        plan.append((done + per + 1, lambda p=p: pass_out(p)))
        plan.append((done + 2 * per + 2, lambda p=p: last_end(p)))
        plan.append((done + 33.7, lambda p=p: pass_in(0, c_mid2, p)))
        plan.append((done + 33.7 + per + 1, lambda p=p: last_mid(p)))
    for _, fn in sorted(plan, key=lambda e: e[0]):
        fn()

    for s in range(1, 8):
        q = peer(s)
        rarrived(y_out.at[block(q), :], 20 + s - 1)
        rarrived(dx_out.at[block(q), :], 27 + s - 1)
        for p in range(PIECES):
            c = rcopy(outs.at[2, piece(p), cols(q)], dw_out.at[q, piece(p)], fin_send.at[s, p], fin_recv.at[s, p], (z, q))
            c.wait_send()
            c.wait_recv()
    for p in range(PIECES):
        pltpu.make_async_copy(outs.at[2, piece(p), cols(t)], dw_out.at[t, piece(p)], fin_send.at[0, p]).wait()
    for c in loc[6:]:
        c.wait()
    skip = set(id(c) for c in x_sends)
    for c in pending:
        if id(c) not in skip:
            c.wait_send()
    for away, r0, base in ((m_away, m0, 0), (e_away, e0, 10)):
        for i in range(4):
            rcopy(away.at[i], r0.at[i], red_send.at[base + i], red_recv.at[base + i], (z, pc)).wait_send()

    def sent(k, p, sl):
        for c in wz(k, p, sl, inner):
            c.wait_send()

    @pl.when(is_end)
    def _():
        each_block(lambda p: sent(c_end, p, 3))
        for q in range(3):
            for p in range(PIECES):
                from_end(q, c_mid, p).wait_send()

    @pl.when(is_mid)
    def _():
        def all_sent(p):
            for sl in (0, 1, 2, 4, 5):
                sent(c_mid, p, sl)
        each_block(all_sent)
        for sl in (3, 4, 5):
            for p in range(PIECES):
                sum_copy(outs.at[0, piece(p)], ins.at[0, piece(p)], sl, p, inner).wait_send()


def place_kernel(y_in, dx_in, dw_in, dg_in, y_out, dx_out, dw1_out, dw3_out, dw2_out, dg_out):
    y_out[...] = y_in[...]
    dx_out[...] = dx_in[...]
    for s in range(N_T):
        at = slice(s * LANE, (s + 1) * LANE)
        dw1_out[:, at] = dw_in[s, 0:LANE].T
        dw3_out[:, at] = dw_in[s, LANE:2 * LANE].T
        dw2_out[at, :] = dw_in[s, 2 * LANE:]
    dg_out[...] = jnp.sum(dg_in[...], axis=0, keepdims=True)


def solution(mesh):
    def local_step(x_blk, dy_blk, gain_blk, w1_blk, w3_blk, w2_blk):
        tokens, lane = x_blk.shape
        d = lane * N_T
        f = w1_blk.shape[1] // N_T * N_Z
        rows = tokens // N_T
        gain8 = jnp.broadcast_to(gain_blk[None, :], (8, lane))
        any_spec = pl.BlockSpec(memory_space=pl.ANY)
        vmem = pl.BlockSpec(memory_space=pltpu.VMEM)
        s = jax.ShapeDtypeStruct
        V = pltpu.VMEM
        dma = pltpu.SemaphoreType.DMA
        red = [V((4, rows, d), F32), V((4, rows, d), F32), V((4, rows // 2, d), F32), V((2, rows // 2, d), F32)]
        y, dx, dw, dg = pl.pallas_call(
            step_kernel,
            out_shape=(s((tokens, lane), BF16), s((tokens, lane), BF16), s((N_T, 384, lane), F32), s((8, lane), F32)),
            in_specs=[any_spec] * 6,
            out_specs=[any_spec] * 3 + [vmem],
            scratch_shapes=[
                V((tokens, d), BF16), V((tokens, d), BF16), V((tokens, d), BF16), V((8, d), F32),
                V((d, 2 * f), BF16), V((f, d), BF16), V((tokens, f), BF16), V((lane, tokens), BF16),
                V((2 * lane, tokens), BF16), V((N_Z, 384, d), F32)] + red + red + [
                V((3, 384, d), F32), V((2, 384, d), F32),
                V((rows, d), BF16), V((rows, d), BF16), V((rows, d), BF16), V((8, d), F32),
                V((7, 8, lane), F32), V((4, 8, lane), F32),
                dma((N_PLANE,)), dma((N_PLANE,)), dma((6, N_T, 2)), dma((6, N_T, 2)),
                dma((6, PIECES)), dma((6, PIECES)), dma((8, PIECES)), dma((8, PIECES)),
                dma((N_RED,)), dma((N_RED,)), dma((8,))],
            compiler_params=pltpu.CompilerParams(has_side_effects=True, vmem_limit_bytes=67043328),
            name="step",
        )(x_blk, dy_blk, gain8, w1_blk, w3_blk, w2_blk)
        f_z = w1_blk.shape[1]
        y, dx, dw1, dw3, dw2, dg = pl.pallas_call(
            place_kernel,
            out_shape=(s((tokens, lane), BF16), s((tokens, lane), BF16), s((lane, f_z), F32), s((lane, f_z), F32),
                       s((f_z, lane), F32), s((1, lane), F32)),
            in_specs=[vmem] * 4, out_specs=[vmem] * 6, name="place",
        )(y, dx, dw, dg)
        return y, dx, dw1, dw3, dw2, dg[0]

    return jax.shard_map(
        local_step, mesh=mesh,
        in_specs=(P("ty", "tx"), P("ty", "tx"), P("tx"), P("tx", "ty"), P("tx", "ty"), P("ty", "tx")),
        out_specs=(P("ty", "tx"), P("ty", "tx"), P("tx", "ty"), P("tx", "ty"), P("ty", "tx"), P("tx")),
        check_vma=False)
```

time: 1200 us -> 206 us (0.17)
  waiting for transfers between devices: 1010 us -> 0 us
  Pallas kernels: 0 us -> 202 us
  matrix products: 100 us -> 0 us
  blocking collectives: 59.7 us -> 0 us
  other arithmetic: 19.1 us -> 0 us
  between operations: 14.3 us -> 0.64 us
    reduce_scatter x5 -> x0, waiting for transfers between devices: 696 us -> none  [the longest x1 208 us: local_step(): lax.psum_scatter(contract_cols(dy_all, w_down_blk), 'tx', scatter_dimensi...]
    all_gather x5 -> x0, waiting for transfers between devices: 307 us -> none  [the longest x1 88.2 us: local_step(): d_gate_all = lax.all_gather(d_gate, 'tx', axis=0, tiled=True)]
    pallas_call x0 -> x2, Pallas kernels: none -> 202 us  [the longest x1 198 us: local_step(): pl.pallas_call(step_kernel, out_shape=(s((tokens, lane), BF16), s((tokens...]
    dot_general x9 -> x0, matrix products: 100 us -> none  [the longest x3 36.5 us: contract_cols(): lax.dot_general(left_op, right_op, (((1,), (1,)), ((), ())), preferred_el...]
    psum x3 -> x0, blocking collectives: 59.7 us -> none  [the longest x1 25.6 us: local_step(): lax.psum(jnp.stack([jnp.sum(x_float, axis=1), jnp.sum(x_float * x_float,...]
    convert_element_type x3 -> x0, other arithmetic: 15.1 us -> none  [the longest x1 8.54 us: local_step(): d_up = (d_act * gate_swish).astype(jnp.bfloat16)]
  transfers between devices with their start and end apart: 10 -> 0, of which waited for: 10 -> 0; matrix products, arithmetic and copies ran while one was open for 9% -> 0% of each run, Pallas kernels for 0% -> 0%
where the time goes in v2:
time: 206 us; the launch traced here: 204 us
  Pallas kernels  202 us (98%)
    pallas_call x1, Pallas kernels, local_step(): pl.pallas_call(step_kernel, out_shape=(s((tokens, lane), BF16), s((tokens...  198 us

profile of v2, /device:TPU:0, one launch (start us, length us, event | category | flops | bytes accessed | tf_op | source)
XLA Modules:
  0.0 203.9 jit_solution(2240340397645944214)
XLA Ops:
  0.6 1.2 broadcast_in_dim.2.g_in
  1.9 198.4 %step.1 = (bf16[2048,128]{1,0:T(8,128)(2,1)}, bf16[2048,128]{1,0:T(8,128)(2,1)}, f32[8,384,128]{2,1,0:T(8,128)}, f32[8,128]{1,0:T(8,128)}) custom-call(bf16[2048,128]{1,0:T(8,128)(2,1)} %x_in.1, bf16[2048,128]{1,0:T(8,128)(2,1)} %dy_in.1, f32[8,128]{1,0:T(8,128)} %broadcast_in_dim.2.g_in, bf16[128,1024]{1,0:T(8,128)(2,1)} %w1_in.1, bf16[128,1024]{1,0:T(8,128)(2,1)} %w3_in.1, ...), custom_call_target="tpu_custom_call" | custom-call | tf_op jit(solution)/shard_map/step/pallas_call | solution.py:535
  200.3 3.5 %place.1 = (bf16[2048,128]{1,0:T(8,128)(2,1)}, bf16[2048,128]{1,0:T(8,128)(2,1)}, f32[128,1024]{1,0:T(8,128)}, f32[128,1024]{1,0:T(8,128)}, f32[1024,128]{1,0:T(8,128)}, /*index=5*/f32[1,128]{1,0:T(1,128)}) custom-call(bf16[2048,128]{1,0:T(8,128)(2,1)} %get-tuple-element.16.y_in, bf16[2048,128]{1,0:T(8,128)(2,1)} %get-tuple-element.17.dx_in, ...), custom_call_target="tpu_custom_call" | custom-call | tf_op jit(solution)/shard_map/place/pallas_call | solution.py:554

commit v3 on v2

--- a/solution.py
+++ b/solution.py
@@ -14,6 +14,7 @@
 N_Z = 4
 PIECES = 6
 ROWS = 384 // PIECES
+PIECE_ORDER = tuple(range(PIECES * 2 // 3, PIECES)) + tuple(range(PIECES * 2 // 3))
 
 
 def cols(k, width=LANE):
@@ -35,8 +36,8 @@
 
 def step_kernel(x_in, dy_in, g_in, w1_in, w3_in, w2_in,
                 y_out, dx_out, dw_out, dg_out,
-                x_all, h_all, dy_all, gain_all, w13, w2, act, act_t, duv_t, dw,
-                m_away, m0, m1, m2, e_away, e0, e1, e2, outs, ins,
+                x_all, h_all, dy_all, gain_all, w13, w2, act, act_t, duv_t, dw, uv_all,
+                m_away, m0, m1, m2, e0, e1, e2, outs, ins,
                 x_rows, y_rows, dx_rows, dg_rows, dg_plane, dg_line,
                 send_sem, recv_sem, wz_send, wz_recv, sum_send, sum_recv, fin_send, fin_recv,
                 red_send, red_recv, local_sem):
@@ -47,6 +48,7 @@
     ybit = lax.div(t, 4)
     flips = (1 - 2 * core, 2 - 4 * xbit, 4 - 8 * ybit)
     duv = x_all
+    e_away = uv_all.at[pl.ds(4, 4)]
 
     def peer(s):
         out = t
@@ -103,6 +105,12 @@
     ]
     for c in loc:
         c.start()
+    barrier = pltpu.get_barrier_semaphore()
+    for s in order:
+        pl.semaphore_signal(barrier, inc=1, device_id=(z, peer(s)), device_id_type=MESH)
+    for s in range(1, N_Z):
+        pl.semaphore_signal(barrier, inc=1, device_id=(lax.rem(z + s, N_Z), t), device_id_type=MESH)
+    pl.semaphore_wait(barrier, N_T - 1 + N_Z - 1)
 
     w_slots = {}
     for s in order:
@@ -133,9 +141,9 @@
         arrived(b, sl[2])
         return out + [forward(b, sl[6], px), forward(b, sl[9], pc)]
 
-    def plane_rest(full, sl):
+    def plane_rest(full, sl, first, n=2):
         out = []
-        for rr, p, i, o in ((hi, px, 1, 8), (lo, py, 3, 10), (lo, pd, 5, 11), (hi, pd, 6, 12)):
+        for rr, p, i, o in ((hi, px, 1, 8), (lo, py, 3, 10), (lo, pd, 5, 11), (hi, pd, 6, 12))[first:first + n]:
             ref = full.at[rr, cols(p)]
             arrived(ref, sl[i])
             out.append(forward(ref, sl[o], pc))
@@ -205,7 +213,7 @@
     def _():
         each_block(hop_one)
 
-    x_sends += plane_rest(x_all, sx)
+    x_sends += plane_rest(x_all, sx, 0, 4)
     for c in loc[3:5]:
         c.wait()
     plane_last(x_all, sx)
@@ -226,80 +234,103 @@
     def block(p):
         return pl.ds(pl.multiple_of(p * rows, rows), rows)
 
+    def piece(p):
+        return pl.ds(p * ROWS, ROWS)
+
+    def sum_copy(src, dst, sl, p, device):
+        return rcopy(src, dst, sum_send.at[sl, p], sum_recv.at[sl, p], (device, t))
+
+    def from_end(q, k, p):
+        return sum_copy(dw.at[k, piece(p)], outs.at[q, piece(p)], q, p, inner)
+
+    def end_send(q, k, pieces):
+        @pl.when(is_end)
+        def _():
+            for p in pieces:
+                from_end(q, k, p).start()
+
+    def uv_tile(i, j):
+        return 2 * i + lax.div(j, 4), cols(lax.rem(j, 4), 2 * LANE)
+
+    def forward_chunk(i, k, sl):
+        if sl is not None:
+            @pl.when(is_end)
+            def _():
+                each_block(lambda p: wz_wait(k, p, sl))
+
+        def tile(j, c):
+            rr = block(j)
+            uv = dot(h_all[rr, :], w13[:, cols(k, 2 * LANE)])
+            at, cc = uv_tile(i, j)
+            uv_all[at, :, cc] = uv
+            u, v = uv[:, :LANE], uv[:, LANE:]
+            act[rr, cols(k)] = (u * jax.nn.sigmoid(u) * v).astype(BF16)
+            return c
+
+        lax.fori_loop(0, N_T, tile, 0)
+
+    def turn_act(k):
+        def tile(j, c):
+            act_t[:, block(j)] = act[block(j), cols(k)].T
+            return c
+        lax.fori_loop(0, N_T, tile, 0)
+
+    n_cols = dy_all.shape[1] // (2 * LANE)
+
+    def grad_down(k):
+        def grad(n, c):
+            nn = cols(n, 2 * LANE)
+            dw[k, 2 * LANE:, nn] = dot(act_t[...], dy_all[:, nn])
+            return c
+        lax.fori_loop(0, n_cols, grad, 0)
+
+    def backward_chunk(i, k):
+        def tile(j, c):
+            rr = block(j)
+            da = dot_cols(dy_all[rr, :], w2[cols(k), :])
+            at, cc = uv_tile(i, j)
+            uv = uv_all[at, :, cc]
+            u, v = uv[:, :LANE], uv[:, LANE:]
+            sig = jax.nn.sigmoid(u)
+            du = (da * v * sig * (1.0 + u * (1.0 - sig))).astype(BF16)
+            dv = (da * (u * sig)).astype(BF16)
+            duv[rr, cols(2 * k)] = du
+            duv[rr, cols(2 * k + 1)] = dv
+            duv_t[0:LANE, rr] = du.T
+            duv_t[LANE:, rr] = dv.T
+            return c
+
+        lax.fori_loop(0, N_T, tile, 0)
+
+        def grad(n, c):
+            nn = cols(n, 2 * LANE)
+            dw[k, 0:2 * LANE, nn] = dot(duv_t[...], h_all[:, nn])
+            return c
+
+        lax.fori_loop(0, n_cols, grad, 0)
+
     lax.fori_loop(0, N_T, norm_tile, 0)
     x_rows[...] = x_all[block(t), :]
+    forward_chunk(0, c_mid, 0)
     plane_forward(dy_all, sd)
 
     @pl.when(is_mid)
     def _():
         each_block(hop_two)
 
-    plane_rest(dy_all, sd)
+    forward_chunk(1, c_end, None)
+    turn_act(c_mid)
+    plane_rest(dy_all, sd, 0)
+    forward_chunk(2, c_mid2, 1)
+    plane_rest(dy_all, sd, 2)
     loc[5].wait()
     plane_last(dy_all, sd)
     for c in x_sends:
         c.wait_send()
-
-    def piece(p):
-        return pl.ds(p * ROWS, ROWS)
-
-    def sum_copy(src, dst, sl, p, device):
-        return rcopy(src, dst, sum_send.at[sl, p], sum_recv.at[sl, p], (device, t))
-
-    def from_end(q, k, p):
-        return sum_copy(dw.at[k, piece(p)], outs.at[q, piece(p)], q, p, inner)
-
-    def end_send(q, k):
-        @pl.when(is_end)
-        def _():
-            for p in range(PIECES):
-                from_end(q, k, p).start()
-
-    def chunk_step(i, carry):
-        b = i + (1 - 2 * lax.rem(i, 2)) * (1 - lax.div(i, 2))
-        k = low * b + (1 - low) * (3 - b)
-
-        for step, sl in ((0, 0), (2, 1), (3, 2)):
-            @pl.when(jnp.logical_and(is_end, i == step))
-            def _(sl=sl):
-                each_block(lambda p: wz_wait(k, p, sl))
-
-        def tile(j, c):
-            rr = block(j)
-            uv = dot(h_all[rr, :], w13[:, cols(k, 2 * LANE)])
-            da = dot_cols(dy_all[rr, :], w2[cols(k), :])
-            u, v = uv[:, :LANE], uv[:, LANE:]
-            sig = jax.nn.sigmoid(u)
-            swish = u * sig
-            a = (swish * v).astype(BF16)
-            du = (da * v * sig * (1.0 + u * (1.0 - sig))).astype(BF16)
-            dv = (da * swish).astype(BF16)
-            act[rr, cols(k)] = a
-            duv[rr, cols(2 * k)] = du
-            duv[rr, cols(2 * k + 1)] = dv
-            act_t[:, rr] = a.T
-            duv_t[0:LANE, rr] = du.T
-            duv_t[LANE:, rr] = dv.T
-            return c
-
-        lax.fori_loop(0, N_T, tile, 0)
-
-        def grad(n, c):
-            nn = cols(n, 2 * LANE)
-            dw[k, 0:2 * LANE, nn] = dot(duv_t[...], h_all[:, nn])
-            dw[k, 2 * LANE:, nn] = dot(act_t[...], dy_all[:, nn])
-            return c
-
-        lax.fori_loop(0, dy_all.shape[1] // (2 * LANE), grad, 0)
-
-        @pl.when(i == 0)
-        def _():
-            end_send(2, c_mid)
-        return carry
-
-    lax.fori_loop(0, N_Z, chunk_step, 0)
-    end_send(1, c_end2)
-    end_send(0, c_mid2)
+    grad_down(c_mid)
+    end_send(2, c_mid, PIECE_ORDER[:2])
+    backward_chunk(0, c_mid)
+    end_send(2, c_mid, PIECE_ORDER[2:])
 
     def stage0(away, r0, make, base):
         def body(j, c):
@@ -310,15 +341,6 @@
             return c
         lax.fori_loop(0, 4, body, 0)
 
-    def stage1(r0, make, base):
-        def body(j, c):
-            fx, fy = 1 - lax.div(j, 2), 1 - lax.rem(j, 2)
-            i = fx + 2 * fy
-            rcopy(r0.at[i], r0.at[i], red_send.at[base + i], red_recv.at[base + i], (z, pc)).wait_recv()
-            r0[i] += make(block(t + fx * flips[1] + fy * flips[2]))
-            return c
-        lax.fori_loop(0, 4, body, 0)
-
     def rsend(src, dst, sl, device):
         c = rcopy(src, dst, red_send.at[sl], red_recv.at[sl], device)
         c.start()
@@ -329,11 +351,17 @@
 
     a_half, b_half = pl.ds(0, hr), pl.ds(hr, hr)
 
-    def stage1_send(r0, r1, base):
-        rsend(r0.at[3, a_half], r1.at[0], base + 4, (z, px))
-        rsend(r0.at[3, b_half], r1.at[1], base + 5, (z, py))
-        rsend(r0.at[1, a_half], r1.at[2], base + 6, (z, px))
-        rsend(r0.at[2, b_half], r1.at[3], base + 7, (z, py))
+    def stage1(r0, r1, make, base):
+        for i in (3, 1, 2, 0):
+            rcopy(r0.at[i], r0.at[i], red_send.at[base + i], red_recv.at[base + i], (z, pc)).wait_recv()
+            r0[i] += make(block((t, px, py, pd)[i]))
+            if i == 3:
+                rsend(r0.at[3, a_half], r1.at[0], base + 4, (z, px))
+                rsend(r0.at[3, b_half], r1.at[1], base + 5, (z, py))
+            if i == 1:
+                rsend(r0.at[1, a_half], r1.at[2], base + 6, (z, px))
+            if i == 2:
+                rsend(r0.at[2, b_half], r1.at[3], base + 7, (z, py))
 
     def stage2(r0, r1, r2, base):
         rarrived(r1.at[0], base + 4)
@@ -361,12 +389,22 @@
     def make_dh(rr):
         return dot_cols(duv[rr, :], w13[...])
 
+    def rest_of_chunk(i, k):
+        turn_act(k)
+        grad_down(k)
+        backward_chunk(i, k)
+
+    forward_chunk(3, c_end2, 2)
     stage0(m_away, m0, make_m, 0)
+    stage1(m0, m1, make_m, 0)
+    rest_of_chunk(3, c_end2)
+    end_send(1, c_end2, PIECE_ORDER)
+    rest_of_chunk(1, c_end)
+    stage2(m0, m1, m2, 0)
+    rest_of_chunk(2, c_mid2)
+    end_send(0, c_mid2, PIECE_ORDER)
     stage0(e_away, e0, make_dh, 10)
-    stage1(m0, make_m, 0)
-    stage1_send(m0, m1, 0)
-    stage1(e0, make_dh, 10)
-    stage1_send(e0, e1, 10)
+    stage1(e0, e1, make_dh, 10)
 
     def finish(src, p):
         for s in (6, 7, 2, 4, 3, 5, 1):
@@ -433,9 +471,9 @@
         dy_rows = dy_all[block(t), :].astype(F32)
         dx_rows[...] = (dy_rows + r * (e - e_mean - xhat * ex_mean)).astype(BF16)
         dg_rows[...] = jnp.sum((dh * xhat).reshape(rows // 8, 8, d), axis=0)
-        spread(dx_rows, dx_out, 27, 7)
         for s in order:
             rsend(dg_rows.at[:, cols(peer(s))], dg_plane.at[s - 1], 34 + s - 1, (z, peer(s)))
+        spread(dx_rows, dx_out, 27, 7)
 
     def gain_plane():
         total = dg_rows[:, cols(t)]
@@ -453,11 +491,11 @@
         dg_out[...] = (parts[0] + parts[1]) + (parts[2] + parts[3])
 
     per = 33.7 / PIECES
-    plan = [(90, lambda: stage2(m0, m1, m2, 0)), (101, lambda: stage3(m0, m1, 0)),
-            (113, lambda: stage2(e0, e1, e2, 10)), (124, lambda: stage3(e0, e1, 10)),
-            (135, make_y), (147, make_dx), (151, gain_plane), (157, gain_line)]
-    for p in range(PIECES):
-        done = 83 + per * (p + 1)
+    plan = [(86, lambda: stage3(m0, m1, 0)), (97, make_y),
+            (111, lambda: stage2(e0, e1, e2, 10)), (122, lambda: stage3(e0, e1, 10)),
+            (135, make_dx), (143, gain_plane), (157, gain_line)]
+    for n, p in enumerate(PIECE_ORDER):
+        done = 88 + per * (n + 1)
         plan.append((done, lambda p=p: pass_in(1, c_end2, p)))
         plan.append((done + per + 1, lambda p=p: pass_out(p)))
         plan.append((done + 2 * per + 2, lambda p=p: last_end(p)))
@@ -525,7 +563,6 @@
         d = lane * N_T
         f = w1_blk.shape[1] // N_T * N_Z
         rows = tokens // N_T
-        gain8 = jnp.broadcast_to(gain_blk[None, :], (8, lane))
         any_spec = pl.BlockSpec(memory_space=pl.ANY)
         vmem = pl.BlockSpec(memory_space=pltpu.VMEM)
         s = jax.ShapeDtypeStruct
@@ -538,18 +575,18 @@
             in_specs=[any_spec] * 6,
             out_specs=[any_spec] * 3 + [vmem],
             scratch_shapes=[
-                V((tokens, d), BF16), V((tokens, d), BF16), V((tokens, d), BF16), V((8, d), F32),
+                V((tokens, d), BF16), V((tokens, d), BF16), V((tokens, d), BF16), V((1, d), F32),
                 V((d, 2 * f), BF16), V((f, d), BF16), V((tokens, f), BF16), V((lane, tokens), BF16),
-                V((2 * lane, tokens), BF16), V((N_Z, 384, d), F32)] + red + red + [
+                V((2 * lane, tokens), BF16), V((N_Z, 384, d), F32), V((N_T, rows, d), F32)] + red + red[1:] + [
                 V((3, 384, d), F32), V((2, 384, d), F32),
                 V((rows, d), BF16), V((rows, d), BF16), V((rows, d), BF16), V((8, d), F32),
                 V((7, 8, lane), F32), V((4, 8, lane), F32),
                 dma((N_PLANE,)), dma((N_PLANE,)), dma((6, N_T, 2)), dma((6, N_T, 2)),
                 dma((6, PIECES)), dma((6, PIECES)), dma((8, PIECES)), dma((8, PIECES)),
                 dma((N_RED,)), dma((N_RED,)), dma((8,))],
-            compiler_params=pltpu.CompilerParams(has_side_effects=True, vmem_limit_bytes=67043328),
+            compiler_params=pltpu.CompilerParams(collective_id=0, has_side_effects=True, vmem_limit_bytes=67043328),
             name="step",
-        )(x_blk, dy_blk, gain8, w1_blk, w3_blk, w2_blk)
+        )(x_blk, dy_blk, gain_blk[None, :], w1_blk, w3_blk, w2_blk)
         f_z = w1_blk.shape[1]
         y, dx, dw1, dw3, dw2, dg = pl.pallas_call(
             place_kernel,

time: 206 us -> 179 us (0.87)
  the two profiles are of different devices: /device:TPU:0 before, /device:TPU:9 now
where the time goes in v3:
time: 179 us
  Pallas kernels  178 us (99%)
    pallas_call x1, Pallas kernels, local_step(): pl.pallas_call(step_kernel, out_shape=(s((tokens, lane), BF16), s((tokens...  175 us

profile of v3, /device:TPU:9, one launch (start us, length us, event | category | flops | bytes accessed | tf_op | source)
XLA Modules:
  0.0 178.9 jit_solution(16402793850318500751)
XLA Ops:
  0.6 174.7 %step.1 = (bf16[2048,128]{1,0:T(8,128)(2,1)}, bf16[2048,128]{1,0:T(8,128)(2,1)}, f32[8,384,128]{2,1,0:T(8,128)}, f32[8,128]{1,0:T(8,128)}) custom-call(bf16[2048,128]{1,0:T(8,128)(2,1)} %x_in.1, bf16[2048,128]{1,0:T(8,128)(2,1)} %dy_in.1, f32[1,128]{1,0:T(1,128)} %bitcast.2, bf16[128,1024]{1,0:T(8,128)(2,1)} %w1_in.1, bf16[128,1024]{1,0:T(8,128)(2,1)} %w3_in.1, ...), custom_call_target="tpu_custom_call" | custom-call | tf_op jit(solution)/shard_map/step/pallas_call | solution.py:572
  175.4 3.5 %place.1 = (bf16[2048,128]{1,0:T(8,128)(2,1)}, bf16[2048,128]{1,0:T(8,128)(2,1)}, f32[128,1024]{1,0:T(8,128)}, f32[128,1024]{1,0:T(8,128)}, f32[1024,128]{1,0:T(8,128)}, /*index=5*/f32[1,128]{1,0:T(1,128)}) custom-call(bf16[2048,128]{1,0:T(8,128)(2,1)} %get-tuple-element.16.y_in, bf16[2048,128]{1,0:T(8,128)(2,1)} %get-tuple-element.17.dx_in, ...), custom_call_target="tpu_custom_call" | custom-call | tf_op jit(solution)/shard_map/place/pallas_call | solution.py:591

commit v4 on v3

v4 whole, which is shorter than its diff:
```python
import jax
import jax.numpy as jnp
from jax import lax
from jax.experimental import pallas as pl
from jax.experimental.pallas import tpu as pltpu
from jax.sharding import PartitionSpec as P

LN_EPS = 1e-6
F32 = jnp.float32
BF16 = jnp.bfloat16
MESH = pl.DeviceIdType.MESH
LANE = 128
N_T = 8
N_Z = 4
PIECES = 6
ROWS = 384 // PIECES
PIECE_ORDER = tuple(range(PIECES * 2 // 3, PIECES)) + tuple(range(PIECES * 2 // 3))


def cols(k, width=LANE):
    return pl.ds(pl.multiple_of(k * width, width), width)


def dot(a, b):
    return jnp.dot(a, b, preferred_element_type=F32)


def dot_cols(a, b):
    return lax.dot_general(a, b, (((1,), (1,)), ((), ())), preferred_element_type=F32)


def step_kernel(x_in, dy_in, g_in, w1_in, w3_in, w2_in,
                y_out, dx_out, dw_out, dg_out,
                x_all, h_all, dy_all, gain_all, w13, w2, act, act_t, duv_t, dw, uv_all,
                m_away, m0, m1, m2, e0, e1, e2, outs, ins,
                x_rows, y_rows, dx_rows, dg_rows, dg_plane, dg_line,
                w_send, w_recv, g_recv, in_send, in_recv, wz_send, wz_end, wz_mid, sum_send, sum_recv,
                fin_sem, red_send, red_recv, local_sem):
    z = lax.axis_index("ty")
    t = lax.axis_index("tx")
    core = lax.rem(t, 2)
    xbit = lax.rem(lax.div(t, 2), 2)
    ybit = lax.div(t, 4)
    flips = (1 - 2 * core, 2 - 4 * xbit, 4 - 8 * ybit)
    duv = x_all
    e_away = uv_all.at[pl.ds(4, 4)]

    def peer(s):
        out = t
        for bit in range(3):
            if s >> bit & 1:
                out = out + flips[bit]
        return out

    px, py, pd, pc = peer(2), peer(4), peer(6), peer(1)
    order = (2, 4, 3, 5, 6, 7, 1)
    tokens = x_all.shape[0]
    half = tokens // 2
    rows = tokens // N_T
    hr = rows // 2

    low = lax.div(3 - z, 2)
    is_end = jnp.logical_or(z == 0, z == 3)
    is_mid = jnp.logical_or(z == 1, z == 2)
    c_end = 3 - 3 * low
    c_mid = 2 - low
    c_mid2 = 3 - c_mid
    c_end2 = 3 - c_end
    inner = z + 2 * low - 1
    outer = z - 2 * low + 1

    def rcopy(src, dst, ssem, rsem, device):
        return pltpu.make_async_remote_copy(src_ref=src, dst_ref=dst, send_sem=ssem, recv_sem=rsem,
                                            device_id=device, device_id_type=MESH)

    def wait_sent(ref, sem):
        rcopy(ref, ref, sem, sem, (z, pc)).wait_send()

    def wait_in(ref, sem):
        rcopy(ref, ref, sem, sem, (z, pc)).wait_recv()

    loc = [
        pltpu.make_async_copy(w1_in.at[:, cols(t)], w13.at[cols(t), cols(2 * z)], local_sem.at[0]),
        pltpu.make_async_copy(w3_in.at[:, cols(t)], w13.at[cols(t), cols(2 * z + 1)], local_sem.at[1]),
        pltpu.make_async_copy(w2_in.at[cols(t), :], w2.at[cols(z), cols(t)], local_sem.at[2]),
        pltpu.make_async_copy(g_in, gain_all.at[:, cols(t)], local_sem.at[3]),
        pltpu.make_async_copy(x_in, x_all.at[:, cols(t)], local_sem.at[4]),
        pltpu.make_async_copy(dy_in, dy_all.at[:, cols(t)], local_sem.at[5]),
    ]
    for c in loc:
        c.start()
    barrier = pltpu.get_barrier_semaphore()
    for s in order:
        pl.semaphore_signal(barrier, inc=1, device_id=(z, peer(s)), device_id_type=MESH)
    for s in range(1, N_Z):
        pl.semaphore_signal(barrier, inc=1, device_id=(lax.rem(z + s, N_Z), t), device_id_type=MESH)
    pl.semaphore_wait(barrier, N_T - 1 + N_Z - 1)

    for s in order:
        p = peer(s)
        rcopy(w1_in.at[:, cols(p)], w13.at[cols(t), cols(2 * z)], w_send.at[0], w_recv.at[s, 0], (z, p)).start()
        rcopy(w3_in.at[:, cols(p)], w13.at[cols(t), cols(2 * z + 1)], w_send.at[1], w_recv.at[s, 0], (z, p)).start()
        rcopy(w2_in.at[cols(p), :], w2.at[cols(z), cols(t)], w_send.at[2], w_recv.at[s, 1], (z, p)).start()
        rcopy(g_in, gain_all.at[:, cols(t)], w_send.at[3], g_recv.at[0], (z, p)).start()

    lo, hi = pl.ds(0, half), pl.ds(half, half)

    def move(n, src, dst, i, device):
        rcopy(src, dst, in_send.at[n], in_recv.at[n, i], (z, device)).start()

    def plane_first(n, src, full):
        move(n, src.at[lo], full.at[lo, cols(t)], 0, px)
        move(n, src.at[hi], full.at[hi, cols(t)], 2, py)
        move(n, src.at[hi], full.at[hi, cols(t)], 1, px)
        move(n, src.at[lo], full.at[lo, cols(t)], 3, py)
        move(n, src, full.at[:, cols(t)], 6, pc)

    def plane_forward(n, full):
        a, b = full.at[lo, cols(px)], full.at[hi, cols(py)]
        wait_in(a, in_recv.at[n, 0])
        move(n, a, a, 4, py)
        move(n, a, a, 6, pc)
        wait_in(b, in_recv.at[n, 2])
        move(n, b, b, 5, px)
        move(n, b, b, 6, pc)

    def plane_rest(n, full, first, many=2):
        for rr, p, i in ((hi, px, 1), (lo, py, 3), (lo, pd, 4), (hi, pd, 5))[first:first + many]:
            ref = full.at[rr, cols(p)]
            wait_in(ref, in_recv.at[n, i])
            move(n, ref, ref, 6, pc)

    def plane_last(n, full):
        wait_in(full.at[:, pl.ds(0, 4 * LANE)], in_recv.at[n, 6])

    plane_first(0, x_in, x_all)

    def wz_one(n, k, p, sl, device, many):
        ref = w2.at[cols(k), cols(p, many * LANE)] if n else w13.at[cols(p, many * LANE), cols(k, 2 * LANE)]
        pair = p if many == 2 else lax.div(p, 2)
        sem = wz_end.at[sl, n] if sl < 3 else wz_mid.at[sl - 3, pair, n]
        return rcopy(ref, ref, wz_send.at[sl, n], sem, (device, t))

    def wz(k, p, sl, device):
        return tuple(wz_one(n, k, p, sl, device, 1) for n in range(2))

    def wz_own(p):
        @pl.when(is_end)
        def _():
            for c in wz(c_end, p, 3, inner):
                c.start()

        @pl.when(is_mid)
        def _():
            for c in wz(c_mid, p, 0, outer) + wz(c_mid, p, 4, inner):
                c.start()

    for c in loc[:3]:
        c.wait()
    wz_own(t)
    for s in (1, 2, 4, 3, 5, 6, 7):
        p = peer(s)
        wait_in(w13.at[cols(p), cols(z, 2 * LANE)], w_recv.at[s, 0])
        wait_in(w2.at[cols(z), cols(p)], w_recv.at[s, 1])
        wz_own(p)

    plane_forward(0, x_all)
    plane_first(1, dy_in, dy_all)

    def each_block(fn):
        lax.fori_loop(0, N_T // 2, lambda p, c: (fn(p), c)[1], 0)

    def pass_weights(n, k, from_sl, to_sl, device):
        def one(p):
            wz_one(n, k, p, from_sl, inner, 2).wait_recv()
            wz_one(n, k, p, to_sl, device, 2).start()
        each_block(one)

    def hop_one():
        pass_weights(0, c_mid2, 4, 1, outer)
        pass_weights(0, c_end, 3, 5, inner)
        pass_weights(1, c_mid2, 4, 1, outer)
        pass_weights(1, c_end, 3, 5, inner)

    def hop_two():
        pass_weights(0, c_end2, 5, 2, outer)

    def hop_three():
        pass_weights(1, c_end2, 5, 2, outer)

    @pl.when(is_mid)
    def _():
        hop_one()

    plane_rest(0, x_all, 0, 4)
    for c in loc[3:5]:
        c.wait()
    wait_in(gain_all.at[:, pl.ds(0, 7 * LANE)], g_recv.at[0])
    plane_last(0, x_all)

    def norm(xf):
        d = xf.shape[1]
        mu = jnp.sum(xf, axis=1, keepdims=True) / d
        sq = jnp.sum(xf * xf, axis=1, keepdims=True) / d
        r = lax.rsqrt(sq - mu * mu + LN_EPS)
        return (xf - mu) * r, r

    def norm_tile(i, carry):
        rr = pl.ds(pl.multiple_of(i * rows, rows), rows)
        xhat, _ = norm(x_all[rr, :].astype(F32))
        h_all[rr, :] = (gain_all[0:1, :] * xhat).astype(BF16)
        return carry

    def block(p):
        return pl.ds(pl.multiple_of(p * rows, rows), rows)

    def piece(p):
        return pl.ds(p * ROWS, ROWS)

    def sum_copy(src, dst, sl, p, device):
        return rcopy(src, dst, sum_send.at[sl], sum_recv.at[sl, p], (device, t))

    def from_end(q, k, p):
        return sum_copy(dw.at[k, piece(p)], outs.at[q, piece(p)], q, p, inner)

    def end_send(q, k, pieces):
        @pl.when(is_end)
        def _():
            for p in pieces:
                from_end(q, k, p).start()

    def uv_tile(i, j):
        return 2 * i + lax.div(j, 4), cols(lax.rem(j, 4), 2 * LANE)

    def forward_chunk(i, k, sl):
        if sl is not None:
            @pl.when(is_end)
            def _():
                wait_in(w13.at[:, cols(k, 2 * LANE)], wz_end.at[sl, 0])

        def tile(j, c):
            rr = block(j)
            uv = dot(h_all[rr, :], w13[:, cols(k, 2 * LANE)])
            at, cc = uv_tile(i, j)
            uv_all[at, :, cc] = uv
            u, v = uv[:, :LANE], uv[:, LANE:]
            act[rr, cols(k)] = (u * jax.nn.sigmoid(u) * v).astype(BF16)
            return c

        lax.fori_loop(0, N_T, tile, 0)

    def turn_act(k):
        def tile(j, c):
            act_t[:, block(j)] = act[block(j), cols(k)].T
            return c
        lax.fori_loop(0, N_T, tile, 0)

    n_cols = dy_all.shape[1] // (2 * LANE)

    def grad_down(k):
        def grad(n, c):
            nn = cols(n, 2 * LANE)
            dw[k, 2 * LANE:, nn] = dot(act_t[...], dy_all[:, nn])
            return c
        lax.fori_loop(0, n_cols, grad, 0)

    def backward_chunk(i, k):
        def tile(j, c):
            rr = block(j)
            da = dot_cols(dy_all[rr, :], w2[cols(k), :])
            at, cc = uv_tile(i, j)
            uv = uv_all[at, :, cc]
            u, v = uv[:, :LANE], uv[:, LANE:]
            sig = jax.nn.sigmoid(u)
            du = (da * v * sig * (1.0 + u * (1.0 - sig))).astype(BF16)
            dv = (da * (u * sig)).astype(BF16)
            duv[rr, cols(2 * k)] = du
            duv[rr, cols(2 * k + 1)] = dv
            duv_t[0:LANE, rr] = du.T
            duv_t[LANE:, rr] = dv.T
            return c

        lax.fori_loop(0, N_T, tile, 0)

        def grad(n, c):
            nn = cols(n, 2 * LANE)
            dw[k, 0:2 * LANE, nn] = dot(duv_t[...], h_all[:, nn])
            return c

        lax.fori_loop(0, n_cols, grad, 0)

    lax.fori_loop(0, N_T, norm_tile, 0)
    x_rows[...] = x_all[block(t), :]

    @pl.when(is_mid)
    def _():
        hop_two()

    forward_chunk(0, c_mid, 0)
    plane_forward(1, dy_all)
    forward_chunk(1, c_end, None)

    @pl.when(is_mid)
    def _():
        hop_three()

    plane_rest(1, dy_all, 0)
    forward_chunk(2, c_mid2, 1)
    turn_act(c_mid2)
    plane_rest(1, dy_all, 2)
    loc[5].wait()
    plane_last(1, dy_all)
    wait_sent(x_all.at[:, pl.ds(0, 7 * LANE)], in_send.at[0])
    grad_down(c_mid2)
    end_send(0, c_mid2, PIECE_ORDER[:2])
    forward_chunk(3, c_end2, 2)

    @pl.when(is_end)
    def _():
        wait_in(w2.at[cols(c_mid2), :], wz_end.at[1, 1])

    backward_chunk(2, c_mid2)
    end_send(0, c_mid2, PIECE_ORDER[2:])

    @pl.when(is_end)
    def _():
        wait_in(w2.at[cols(c_mid), :], wz_end.at[0, 1])
        wait_in(w2.at[cols(c_end2), :], wz_end.at[2, 1])

    def stage0(away, r0, make, base):
        def body(j, c):
            fx, fy = 1 - lax.div(j, 2), 1 - lax.rem(j, 2)
            i = fx + 2 * fy
            away[i] = make(block(pc + fx * flips[1] + fy * flips[2]))
            rcopy(away.at[i], r0.at[i], red_send.at[base // 10], red_recv.at[base + i], (z, pc)).start()
            return c
        lax.fori_loop(0, 4, body, 0)

    def rsend(src, dst, group, sl, device):
        rcopy(src, dst, red_send.at[group], red_recv.at[sl], device).start()

    def rarrived(dst, sl):
        wait_in(dst, red_recv.at[sl])

    a_half, b_half = pl.ds(0, hr), pl.ds(hr, hr)

    def stage1(r0, r1, make, base, between):
        for i in (3, 1, 2, 0):
            rarrived(r0.at[i], base + i)
            r0[i] += make(block((t, px, py, pd)[i]))
            if i == 3:
                rsend(r0.at[3, a_half], r1.at[0], base // 10, base + 4, (z, px))
                rsend(r0.at[3, b_half], r1.at[1], base // 10, base + 5, (z, py))
            if i == 1:
                rsend(r0.at[1, a_half], r1.at[2], base // 10, base + 6, (z, px))
            if i == 2:
                rsend(r0.at[2, b_half], r1.at[3], base // 10, base + 7, (z, py))
            for p in between.get(i, ()):
                pass_in(0, c_mid2, p)

    def stage2(r0, r1, r2, base):
        rarrived(r1.at[0], base + 4)
        r0[2, 0:hr] += r1[0]
        rsend(r0.at[2, a_half], r2.at[0], base // 10, base + 8, (z, py))
        rarrived(r1.at[1], base + 5)
        r0[1, hr:rows] += r1[1]
        rsend(r0.at[1, b_half], r2.at[1], base // 10, base + 9, (z, px))

    def stage3(r0, r1, base):
        rarrived(r1.at[2], base + 6)
        r0[0, 0:hr] += r1[2]
        rarrived(r1.at[3], base + 7)
        r0[0, hr:rows] += r1[3]

    def stage4(r0, r2, base):
        rarrived(r2.at[0], base + 8)
        r0[0, 0:hr] += r2[0]
        rarrived(r2.at[1], base + 9)
        r0[0, hr:rows] += r2[1]

    def make_m(rr):
        return dot(act[rr, :], w2[...])

    def make_dh(rr):
        return dot_cols(duv[rr, :], w13[...])

    def finish(src, p):
        for s in (6, 7, 2, 4, 3, 5, 1):
            q = peer(s)
            rcopy(src.at[:, cols(q)], dw_out.at[t, piece(p)], fin_sem.at[0], fin_sem.at[1], (z, q)).start()
        pltpu.make_async_copy(src.at[:, cols(t)], dw_out.at[t, piece(p)], fin_sem.at[2]).start()

    def pass_in(q, k, p):
        @pl.when(is_mid)
        def _():
            ref = outs.at[q, piece(p)]
            sum_copy(ref, ref, q, p, outer).wait_recv()
            outs[q, p * ROWS:(p + 1) * ROWS] += dw[k, p * ROWS:(p + 1) * ROWS]
            sum_copy(ref, ins.at[q, piece(p)], 3 + q, p, inner).start()

    def pass_out(p):
        @pl.when(is_mid)
        def _():
            ref = ins.at[1, piece(p)]
            sum_copy(ref, ref, 4, p, inner).wait_recv()
            ins[1, p * ROWS:(p + 1) * ROWS] += dw[c_end, p * ROWS:(p + 1) * ROWS]
            sum_copy(ref, ref, 5, p, outer).start()

    def last_mid(p):
        @pl.when(is_mid)
        def _():
            a, b = outs.at[2, piece(p)], ins.at[0, piece(p)]
            sum_copy(b, b, 3, p, inner).wait_recv()
            sum_copy(a, a, 2, p, outer).wait_recv()
            rr = slice(p * ROWS, (p + 1) * ROWS)
            outs[2, rr] += ins[0, rr] + dw[c_mid, rr]
            finish(a, p)

    def last_end(p):
        @pl.when(is_end)
        def _():
            a = ins.at[1, piece(p)]
            sum_copy(a, a, 5, p, inner).wait_recv()
            rr = slice(p * ROWS, (p + 1) * ROWS)
            ins[1, rr] += dw[c_end, rr]
            finish(a, p)

    stage0(m_away, m0, make_m, 0)
    stage1(m0, m1, make_m, 0, {3: PIECE_ORDER[:1], 2: PIECE_ORDER[1:2]})
    turn_act(c_end2)
    grad_down(c_end2)
    pass_in(0, c_mid2, PIECE_ORDER[2])
    backward_chunk(3, c_end2)
    end_send(1, c_end2, PIECE_ORDER)
    turn_act(c_mid)
    grad_down(c_mid)
    pass_in(0, c_mid2, PIECE_ORDER[3])
    backward_chunk(0, c_mid)
    end_send(2, c_mid, PIECE_ORDER)
    stage2(m0, m1, m2, 0)
    pass_in(0, c_mid2, PIECE_ORDER[4])
    turn_act(c_end)
    grad_down(c_end)
    backward_chunk(1, c_end)
    pass_in(0, c_mid2, PIECE_ORDER[5])
    stage0(e_away, e0, make_dh, 10)
    stage1(e0, e1, make_dh, 10, {})

    def spread(src, dst, group, local):
        for s in (6, 7, 2, 4, 3, 5, 1):
            q = peer(s)
            rsend(src.at[:, cols(q)], dst.at[block(t), :], group, group + 18, (z, q))
        c = pltpu.make_async_copy(src.at[:, cols(t)], dst.at[block(t), :], local_sem.at[local])
        c.start()
        loc.append(c)

    def make_y():
        stage4(m0, m2, 0)
        y_rows[...] = (x_rows[...].astype(F32) + m0[0]).astype(BF16)
        spread(y_rows, y_out, 2, 6)

    def make_dx():
        stage4(e0, e2, 10)
        xhat, r = norm(x_rows[...].astype(F32))
        d = xhat.shape[1]
        dh = e0[0]
        e = dh * gain_all[0:1, :]
        e_mean = jnp.sum(e, axis=1, keepdims=True) / d
        ex_mean = jnp.sum(e * xhat, axis=1, keepdims=True) / d
        dy_rows = dy_all[block(t), :].astype(F32)
        dx_rows[...] = (dy_rows + r * (e - e_mean - xhat * ex_mean)).astype(BF16)
        dg_rows[...] = jnp.sum((dh * xhat).reshape(rows // 8, 8, d), axis=0)
        for s in order:
            rsend(dg_rows.at[:, cols(peer(s))], dg_plane.at[s - 1], 4, 22, (z, peer(s)))
        spread(dx_rows, dx_out, 3, 7)

    def gain_plane():
        total = dg_rows[:, cols(t)]
        rarrived(dg_plane, 22)
        for s in range(1, 8):
            total = total + dg_plane[s - 1]
        dg_line[0] = total
        for s in range(1, 4):
            rsend(dg_line.at[0], dg_line.at[s], 5, 23, (lax.rem(z + s, 4), t))

    def gain_line():
        rarrived(dg_line.at[pl.ds(1, 3)], 23)
        parts = [dg_line[lax.rem(z - s + 4, 4)] for s in range(4)]
        dg_out[...] = (parts[0] + parts[1]) + (parts[2] + parts[3])

    per = 33.7 / PIECES
    plan = [(84, lambda: stage3(m0, m1, 0)), (108.6, make_y),
            (108.5, lambda: stage2(e0, e1, e2, 10)), (121, lambda: stage3(e0, e1, 10)),
            (131, make_dx), (149.5, gain_plane), (157, gain_line)]
    for n, p in enumerate(PIECE_ORDER):
        done = 86 + per * (n + 1)
        plan.append((done, lambda p=p: pass_in(1, c_end2, p)))
        plan.append((done + per + 1, lambda p=p: pass_out(p)))
        plan.append((done + 2 * per + 2, lambda p=p: last_end(p)))
        plan.append((done + 33.7, lambda p=p: last_mid(p)))
    for _, fn in sorted(plan, key=lambda e: e[0]):
        fn()

    seven = pl.ds(0, 7 * LANE)
    rarrived(y_out.at[pl.ds(0, 7 * rows), :], 20)
    rarrived(dx_out.at[pl.ds(0, 7 * rows), :], 21)
    wait_in(dw_out.at[pl.ds(0, 7)], fin_sem.at[1])
    pltpu.make_async_copy(dw_out.at[0], dw_out.at[0], fin_sem.at[2]).wait()
    for c in loc[6:]:
        c.wait()
    wait_sent(dw_out.at[pl.ds(0, 7)], fin_sem.at[0])
    for n in range(3):
        wait_sent(w13.at[pl.ds(0, LANE), seven], w_send.at[n])
    wait_sent(gain_all.at[:, seven], w_send.at[3])
    wait_sent(dy_all.at[:, seven], in_send.at[1])
    for n, ref in enumerate((uv_all.at[pl.ds(0, 7)], uv_all.at[pl.ds(0, 7)], y_rows.at[:, seven], dx_rows.at[:, seven],
                             dg_rows.at[:, seven], dg_line.at[pl.ds(1, 3)])):
        wait_sent(ref, red_send.at[n])

    def chunk_sent(sl):
        wait_sent(w13.at[:, cols(0, 2 * LANE)], wz_send.at[sl, 0])
        wait_sent(w2.at[cols(0), :], wz_send.at[sl, 1])

    @pl.when(is_end)
    def _():
        chunk_sent(3)
        for q in range(3):
            wait_sent(dw.at[0], sum_send.at[q])

    @pl.when(is_mid)
    def _():
        for sl in (0, 1, 2, 4, 5):
            chunk_sent(sl)
        for q in (3, 4, 5):
            wait_sent(dw.at[0], sum_send.at[q])


def place_kernel(y_in, dx_in, dw_in, dg_in, y_out, dx_out, dw1_out, dw3_out, dw2_out, dg_out):
    y_out[...] = y_in[...]
    dx_out[...] = dx_in[...]
    for s in range(N_T):
        at = slice(s * LANE, (s + 1) * LANE)
        dw1_out[:, at] = dw_in[s, 0:LANE].T
        dw3_out[:, at] = dw_in[s, LANE:2 * LANE].T
        dw2_out[at, :] = dw_in[s, 2 * LANE:]
    dg_out[...] = jnp.sum(dg_in[...], axis=0, keepdims=True)


def solution(mesh):
    def local_step(x_blk, dy_blk, gain_blk, w1_blk, w3_blk, w2_blk):
        tokens, lane = x_blk.shape
        d = lane * N_T
        f = w1_blk.shape[1] // N_T * N_Z
        rows = tokens // N_T
        any_spec = pl.BlockSpec(memory_space=pl.ANY)
        vmem = pl.BlockSpec(memory_space=pltpu.VMEM)
        s = jax.ShapeDtypeStruct
        V = pltpu.VMEM
        dma = pltpu.SemaphoreType.DMA
        red = [V((4, rows, d), F32), V((4, rows, d), F32), V((4, rows // 2, d), F32), V((2, rows // 2, d), F32)]
        y, dx, dw, dg = pl.pallas_call(
            step_kernel,
            out_shape=(s((tokens, lane), BF16), s((tokens, lane), BF16), s((N_T, 384, lane), F32), s((8, lane), F32)),
            in_specs=[any_spec] * 6,
            out_specs=[any_spec] * 3 + [vmem],
            scratch_shapes=[
                V((tokens, d), BF16), V((tokens, d), BF16), V((tokens, d), BF16), V((1, d), F32),
                V((d, 2 * f), BF16), V((f, d), BF16), V((tokens, f), BF16), V((lane, tokens), BF16),
                V((2 * lane, tokens), BF16), V((N_Z, 384, d), F32), V((N_T, rows, d), F32)] + red + red[1:] + [
                V((3, 384, d), F32), V((2, 384, d), F32),
                V((rows, d), BF16), V((rows, d), BF16), V((rows, d), BF16), V((8, d), F32),
                V((7, 8, lane), F32), V((4, 8, lane), F32),
                dma((4,)), dma((N_T, 2)), dma((1,)), dma((2,)), dma((2, 7)), dma((6, 2)), dma((3, 2)),
                dma((3, N_T // 2, 2)), dma((6,)), dma((6, PIECES)), dma((3,)), dma((6,)), dma((24,)), dma((8,))],
            compiler_params=pltpu.CompilerParams(collective_id=0, has_side_effects=True, vmem_limit_bytes=67043328),
            name="step",
        )(x_blk, dy_blk, gain_blk[None, :], w1_blk, w3_blk, w2_blk)
        f_z = w1_blk.shape[1]
        y, dx, dw1, dw3, dw2, dg = pl.pallas_call(
            place_kernel,
            out_shape=(s((tokens, lane), BF16), s((tokens, lane), BF16), s((lane, f_z), F32), s((lane, f_z), F32),
                       s((f_z, lane), F32), s((1, lane), F32)),
            in_specs=[vmem] * 4, out_specs=[vmem] * 6, name="place",
        )(y, dx, dw, dg)
        return y, dx, dw1, dw3, dw2, dg[0]

    return jax.shard_map(
        local_step, mesh=mesh,
        in_specs=(P("ty", "tx"), P("ty", "tx"), P("tx"), P("tx", "ty"), P("tx", "ty"), P("ty", "tx")),
        out_specs=(P("ty", "tx"), P("ty", "tx"), P("tx", "ty"), P("tx", "ty"), P("ty", "tx"), P("tx")),
        check_vma=False)
```

time: 179 us -> 168 us (0.939)
  the two profiles are of different devices: /device:TPU:9 before, /device:TPU:0 now
where the time goes in v4:
time: 168 us
  Pallas kernels  167 us (99%)
    pallas_call x1, Pallas kernels, local_step(): pl.pallas_call(step_kernel, out_shape=(s((tokens, lane), BF16), s((tokens...  164 us
    pallas_call x1, Pallas kernels, local_step(): pl.pallas_call(place_kernel, out_shape=(s((tokens, lane), BF16), s((token...  3.52 us

profile of v4, /device:TPU:0, one launch (start us, length us, event | category | flops | bytes accessed | tf_op | source)
XLA Modules:
  0.0 167.8 jit_solution(8987469052640075255)
XLA Ops:
  0.6 163.6 %step.1 = (bf16[2048,128]{1,0:T(8,128)(2,1)}, bf16[2048,128]{1,0:T(8,128)(2,1)}, f32[8,384,128]{2,1,0:T(8,128)}, f32[8,128]{1,0:T(8,128)}) custom-call(bf16[2048,128]{1,0:T(8,128)(2,1)} %x_in.1, bf16[2048,128]{1,0:T(8,128)(2,1)} %dy_in.1, f32[1,128]{1,0:T(1,128)} %bitcast.2, bf16[128,1024]{1,0:T(8,128)(2,1)} %w1_in.1, bf16[128,1024]{1,0:T(8,128)(2,1)} %w3_in.1, ...), custom_call_target="tpu_custom_call" | custom-call | tf_op jit(solution)/shard_map/step/pallas_call | solution.py:561
  164.3 3.5 %place.1 = (bf16[2048,128]{1,0:T(8,128)(2,1)}, bf16[2048,128]{1,0:T(8,128)(2,1)}, f32[128,1024]{1,0:T(8,128)}, f32[128,1024]{1,0:T(8,128)}, f32[1024,128]{1,0:T(8,128)}, /*index=5*/f32[1,128]{1,0:T(1,128)}) custom-call(bf16[2048,128]{1,0:T(8,128)(2,1)} %get-tuple-element.16.y_in, bf16[2048,128]{1,0:T(8,128)(2,1)} %get-tuple-element.17.dx_in, ...), custom_call_target="tpu_custom_call" | custom-call | tf_op jit(solution)/shard_map/place/pallas_call | solution.py:579

commit v5 on v4

--- a/solution.py
+++ b/solution.py
@@ -10,11 +10,14 @@
 BF16 = jnp.bfloat16
 MESH = pl.DeviceIdType.MESH
 LANE = 128
+WIDE = LANE + LANE
+ORDER = (2, 4, 3, 5, 6, 7, 1)
 N_T = 8
 N_Z = 4
 PIECES = 6
-ROWS = 384 // PIECES
-PIECE_ORDER = tuple(range(PIECES * 2 // 3, PIECES)) + tuple(range(PIECES * 2 // 3))
+CHUNK = 3 * LANE
+ROWS = CHUNK // PIECES
+PIECE_ORDER = (4, 5, 0, 1, 2, 3)
 
 
 def cols(k, width=LANE):
@@ -41,7 +44,7 @@
     core = lax.rem(t, 2)
     xbit = lax.rem(lax.div(t, 2), 2)
     ybit = lax.div(t, 4)
-    flips = (1 - 2 * core, 2 - 4 * xbit, 4 - 8 * ybit)
+    flips = [size - 2 * size * bit for size, bit in ((1, core), (2, xbit), (4, ybit))]
     duv = x_all
     e_away = uv_all.at[pl.ds(4, 4)]
 
@@ -53,7 +56,6 @@
         return out
 
     px, py, pd, pc = peer(2), peer(4), peer(6), peer(1)
-    order = (2, 4, 3, 5, 6, 7, 1)
     tokens = x_all.shape[0]
     half = tokens // 2
     rows = tokens // N_T
@@ -90,13 +92,13 @@
     for c in loc:
         c.start()
     barrier = pltpu.get_barrier_semaphore()
-    for s in order:
+    for s in ORDER:
         pl.semaphore_signal(barrier, inc=1, device_id=(z, peer(s)), device_id_type=MESH)
     for s in range(1, N_Z):
         pl.semaphore_signal(barrier, inc=1, device_id=(lax.rem(z + s, N_Z), t), device_id_type=MESH)
     pl.semaphore_wait(barrier, N_T - 1 + N_Z - 1)
 
-    for s in order:
+    for s in ORDER:
         p = peer(s)
         rcopy(w1_in.at[:, cols(p)], w13.at[cols(t), cols(2 * z)], w_send.at[0], w_recv.at[s, 0], (z, p)).start()
         rcopy(w3_in.at[:, cols(p)], w13.at[cols(t), cols(2 * z + 1)], w_send.at[1], w_recv.at[s, 0], (z, p)).start()
@@ -136,7 +138,7 @@
     plane_first(0, x_in, x_all)
 
     def wz_one(n, k, p, sl, device, many):
-        ref = w2.at[cols(k), cols(p, many * LANE)] if n else w13.at[cols(p, many * LANE), cols(k, 2 * LANE)]
+        ref = w2.at[cols(k), cols(p, many * LANE)] if n else w13.at[cols(p, many * LANE), cols(k, WIDE)]
         pair = p if many == 2 else lax.div(p, 2)
         sem = wz_end.at[sl, n] if sl < 3 else wz_mid.at[sl - 3, pair, n]
         return rcopy(ref, ref, wz_send.at[sl, n], sem, (device, t))
@@ -158,9 +160,9 @@
     for c in loc[:3]:
         c.wait()
     wz_own(t)
-    for s in (1, 2, 4, 3, 5, 6, 7):
+    for s in ORDER[-1:] + ORDER[:-1]:
         p = peer(s)
-        wait_in(w13.at[cols(p), cols(z, 2 * LANE)], w_recv.at[s, 0])
+        wait_in(w13.at[cols(p), cols(z, WIDE)], w_recv.at[s, 0])
         wait_in(w2.at[cols(z), cols(p)], w_recv.at[s, 1])
         wz_own(p)
 
@@ -230,17 +232,17 @@
                 from_end(q, k, p).start()
 
     def uv_tile(i, j):
-        return 2 * i + lax.div(j, 4), cols(lax.rem(j, 4), 2 * LANE)
+        return 2 * i + lax.div(j, 4), cols(lax.rem(j, 4), WIDE)
 
     def forward_chunk(i, k, sl):
         if sl is not None:
             @pl.when(is_end)
             def _():
-                wait_in(w13.at[:, cols(k, 2 * LANE)], wz_end.at[sl, 0])
+                wait_in(w13.at[:, cols(k, WIDE)], wz_end.at[sl, 0])
 
         def tile(j, c):
             rr = block(j)
-            uv = dot(h_all[rr, :], w13[:, cols(k, 2 * LANE)])
+            uv = dot(h_all[rr, :], w13[:, cols(k, WIDE)])
             at, cc = uv_tile(i, j)
             uv_all[at, :, cc] = uv
             u, v = uv[:, :LANE], uv[:, LANE:]
@@ -255,12 +257,12 @@
             return c
         lax.fori_loop(0, N_T, tile, 0)
 
-    n_cols = dy_all.shape[1] // (2 * LANE)
+    n_cols = dy_all.shape[1] // (WIDE)
 
     def grad_down(k):
         def grad(n, c):
-            nn = cols(n, 2 * LANE)
-            dw[k, 2 * LANE:, nn] = dot(act_t[...], dy_all[:, nn])
+            nn = cols(n, WIDE)
+            dw[k, WIDE:, nn] = dot(act_t[...], dy_all[:, nn])
             return c
         lax.fori_loop(0, n_cols, grad, 0)
 
@@ -283,8 +285,8 @@
         lax.fori_loop(0, N_T, tile, 0)
 
         def grad(n, c):
-            nn = cols(n, 2 * LANE)
-            dw[k, 0:2 * LANE, nn] = dot(duv_t[...], h_all[:, nn])
+            nn = cols(n, WIDE)
+            dw[k, 0:WIDE, nn] = dot(duv_t[...], h_all[:, nn])
             return c
 
         lax.fori_loop(0, n_cols, grad, 0)
@@ -385,7 +387,7 @@
         return dot_cols(duv[rr, :], w13[...])
 
     def finish(src, p):
-        for s in (6, 7, 2, 4, 3, 5, 1):
+        for s in ORDER:
             q = peer(s)
             rcopy(src.at[:, cols(q)], dw_out.at[t, piece(p)], fin_sem.at[0], fin_sem.at[1], (z, q)).start()
         pltpu.make_async_copy(src.at[:, cols(t)], dw_out.at[t, piece(p)], fin_sem.at[2]).start()
@@ -395,7 +397,7 @@
         def _():
             ref = outs.at[q, piece(p)]
             sum_copy(ref, ref, q, p, outer).wait_recv()
-            outs[q, p * ROWS:(p + 1) * ROWS] += dw[k, p * ROWS:(p + 1) * ROWS]
+            outs[q, piece(p)] += dw[k, piece(p)]
             sum_copy(ref, ins.at[q, piece(p)], 3 + q, p, inner).start()
 
     def pass_out(p):
@@ -403,7 +405,7 @@
         def _():
             ref = ins.at[1, piece(p)]
             sum_copy(ref, ref, 4, p, inner).wait_recv()
-            ins[1, p * ROWS:(p + 1) * ROWS] += dw[c_end, p * ROWS:(p + 1) * ROWS]
+            ins[1, piece(p)] += dw[c_end, piece(p)]
             sum_copy(ref, ref, 5, p, outer).start()
 
     def last_mid(p):
@@ -412,7 +414,7 @@
             a, b = outs.at[2, piece(p)], ins.at[0, piece(p)]
             sum_copy(b, b, 3, p, inner).wait_recv()
             sum_copy(a, a, 2, p, outer).wait_recv()
-            rr = slice(p * ROWS, (p + 1) * ROWS)
+            rr = piece(p)
             outs[2, rr] += ins[0, rr] + dw[c_mid, rr]
             finish(a, p)
 
@@ -421,7 +423,7 @@
         def _():
             a = ins.at[1, piece(p)]
             sum_copy(a, a, 5, p, inner).wait_recv()
-            rr = slice(p * ROWS, (p + 1) * ROWS)
+            rr = piece(p)
             ins[1, rr] += dw[c_end, rr]
             finish(a, p)
 
@@ -447,7 +449,7 @@
     stage1(e0, e1, make_dh, 10, {})
 
     def spread(src, dst, group, local):
-        for s in (6, 7, 2, 4, 3, 5, 1):
+        for s in ORDER:
             q = peer(s)
             rsend(src.at[:, cols(q)], dst.at[block(t), :], group, group + 18, (z, q))
         c = pltpu.make_async_copy(src.at[:, cols(t)], dst.at[block(t), :], local_sem.at[local])
@@ -470,7 +472,7 @@
         dy_rows = dy_all[block(t), :].astype(F32)
         dx_rows[...] = (dy_rows + r * (e - e_mean - xhat * ex_mean)).astype(BF16)
         dg_rows[...] = jnp.sum((dh * xhat).reshape(rows // 8, 8, d), axis=0)
-        for s in order:
+        for s in ORDER:
             rsend(dg_rows.at[:, cols(peer(s))], dg_plane.at[s - 1], 4, 22, (z, peer(s)))
         spread(dx_rows, dx_out, 3, 7)
 
@@ -486,7 +488,7 @@
     def gain_line():
         rarrived(dg_line.at[pl.ds(1, 3)], 23)
         parts = [dg_line[lax.rem(z - s + 4, 4)] for s in range(4)]
-        dg_out[...] = (parts[0] + parts[1]) + (parts[2] + parts[3])
+        dg_out[...] = sum(parts[1:], parts[0])
 
     per = 33.7 / PIECES
     plan = [(84, lambda: stage3(m0, m1, 0)), (108.6, make_y),
@@ -518,7 +520,7 @@
         wait_sent(ref, red_send.at[n])
 
     def chunk_sent(sl):
-        wait_sent(w13.at[:, cols(0, 2 * LANE)], wz_send.at[sl, 0])
+        wait_sent(w13.at[:, cols(0, WIDE)], wz_send.at[sl, 0])
         wait_sent(w2.at[cols(0), :], wz_send.at[sl, 1])
 
     @pl.when(is_end)
@@ -529,9 +531,10 @@
 
     @pl.when(is_mid)
     def _():
-        for sl in (0, 1, 2, 4, 5):
-            chunk_sent(sl)
-        for q in (3, 4, 5):
+        for sl in range(6):
+            if sl != 3:
+                chunk_sent(sl)
+        for q in range(3, 6):
             wait_sent(dw.at[0], sum_send.at[q])
 
 
@@ -541,8 +544,8 @@
     for s in range(N_T):
         at = slice(s * LANE, (s + 1) * LANE)
         dw1_out[:, at] = dw_in[s, 0:LANE].T
-        dw3_out[:, at] = dw_in[s, LANE:2 * LANE].T
-        dw2_out[at, :] = dw_in[s, 2 * LANE:]
+        dw3_out[:, at] = dw_in[s, LANE:WIDE].T
+        dw2_out[at, :] = dw_in[s, WIDE:]
     dg_out[...] = jnp.sum(dg_in[...], axis=0, keepdims=True)
 
 
@@ -560,14 +563,14 @@
         red = [V((4, rows, d), F32), V((4, rows, d), F32), V((4, rows // 2, d), F32), V((2, rows // 2, d), F32)]
         y, dx, dw, dg = pl.pallas_call(
             step_kernel,
-            out_shape=(s((tokens, lane), BF16), s((tokens, lane), BF16), s((N_T, 384, lane), F32), s((8, lane), F32)),
+            out_shape=(s((tokens, lane), BF16), s((tokens, lane), BF16), s((N_T, CHUNK, lane), F32), s((8, lane), F32)),
             in_specs=[any_spec] * 6,
             out_specs=[any_spec] * 3 + [vmem],
             scratch_shapes=[
                 V((tokens, d), BF16), V((tokens, d), BF16), V((tokens, d), BF16), V((1, d), F32),
                 V((d, 2 * f), BF16), V((f, d), BF16), V((tokens, f), BF16), V((lane, tokens), BF16),
-                V((2 * lane, tokens), BF16), V((N_Z, 384, d), F32), V((N_T, rows, d), F32)] + red + red[1:] + [
-                V((3, 384, d), F32), V((2, 384, d), F32),
+                V((WIDE, tokens), BF16), V((N_Z, CHUNK, d), F32), V((N_T, rows, d), F32)] + red + red[1:] + [
+                V((3, CHUNK, d), F32), V((2, CHUNK, d), F32),
                 V((rows, d), BF16), V((rows, d), BF16), V((rows, d), BF16), V((8, d), F32),
                 V((7, 8, lane), F32), V((4, 8, lane), F32),
                 dma((4,)), dma((N_T, 2)), dma((1,)), dma((2,)), dma((2, 7)), dma((6, 2)), dma((3, 2)),

time: 168 us -> 169 us (level)
  no operation moved by 1% of the time
where the time goes in v5:
time: 169 us
  Pallas kernels  168 us (99%)
    pallas_call x1, Pallas kernels, local_step(): pl.pallas_call(step_kernel, out_shape=(s((tokens, lane), BF16), s((tokens...  164 us
    pallas_call x1, Pallas kernels, local_step(): pl.pallas_call(place_kernel, out_shape=(s((tokens, lane), BF16), s((token...  3.52 us

profile of v5, /device:TPU:0, one launch (start us, length us, event | category | flops | bytes accessed | tf_op | source)
XLA Modules:
  0.0 168.6 jit_solution(15278683204230564607)
XLA Ops:
  0.6 164.4 %step.1 = (bf16[2048,128]{1,0:T(8,128)(2,1)}, bf16[2048,128]{1,0:T(8,128)(2,1)}, f32[8,384,128]{2,1,0:T(8,128)}, f32[8,128]{1,0:T(8,128)}) custom-call(bf16[2048,128]{1,0:T(8,128)(2,1)} %x_in.1, bf16[2048,128]{1,0:T(8,128)(2,1)} %dy_in.1, f32[1,128]{1,0:T(1,128)} %bitcast.2, bf16[128,1024]{1,0:T(8,128)(2,1)} %w1_in.1, bf16[128,1024]{1,0:T(8,128)(2,1)} %w3_in.1, ...), custom_call_target="tpu_custom_call" | custom-call | tf_op jit(solution)/shard_map/step/pallas_call | solution.py:564
  165.1 3.5 %place.1 = (bf16[2048,128]{1,0:T(8,128)(2,1)}, bf16[2048,128]{1,0:T(8,128)(2,1)}, f32[128,1024]{1,0:T(8,128)}, f32[128,1024]{1,0:T(8,128)}, f32[1024,128]{1,0:T(8,128)}, /*index=5*/f32[1,128]{1,0:T(1,128)}) custom-call(bf16[2048,128]{1,0:T(8,128)(2,1)} %get-tuple-element.16.y_in, bf16[2048,128]{1,0:T(8,128)(2,1)} %get-tuple-element.17.dx_in, ...), custom_call_target="tpu_custom_call" | custom-call | tf_op jit(solution)/shard_map/place/pallas_call | solution.py:582

commit v6 on v5

--- a/solution.py
+++ b/solution.py
@@ -14,10 +14,10 @@
 ORDER = (2, 4, 3, 5, 6, 7, 1)
 N_T = 8
 N_Z = 4
-PIECES = 6
+PIECES = 8
 CHUNK = 3 * LANE
-ROWS = CHUNK // PIECES
-PIECE_ORDER = (4, 5, 0, 1, 2, 3)
+ROWS = LANE // 2
+PIECE_ORDER = tuple(range(4, PIECES)) + tuple(range(4))
 
 
 def cols(k, width=LANE):
@@ -36,7 +36,7 @@
                 y_out, dx_out, dw_out, dg_out,
                 x_all, h_all, dy_all, gain_all, w13, w2, act, act_t, duv_t, dw, uv_all,
                 m_away, m0, m1, m2, e0, e1, e2, outs, ins,
-                x_rows, y_rows, dx_rows, dg_rows, dg_plane, dg_line,
+                x_rows, x_own, dg_rows, dg_plane, dg_line,
                 w_send, w_recv, g_recv, in_send, in_recv, wz_send, wz_end, wz_mid, sum_send, sum_recv,
                 fin_sem, red_send, red_recv, local_sem):
     z = lax.axis_index("ty")
@@ -59,7 +59,6 @@
     tokens = x_all.shape[0]
     half = tokens // 2
     rows = tokens // N_T
-    hr = rows // 2
 
     low = lax.div(3 - z, 2)
     is_end = jnp.logical_or(z == 0, z == 3)
@@ -88,6 +87,7 @@
         pltpu.make_async_copy(g_in, gain_all.at[:, cols(t)], local_sem.at[3]),
         pltpu.make_async_copy(x_in, x_all.at[:, cols(t)], local_sem.at[4]),
         pltpu.make_async_copy(dy_in, dy_all.at[:, cols(t)], local_sem.at[5]),
+        pltpu.make_async_copy(x_in, x_own, local_sem.at[8]),
     ]
     for c in loc:
         c.start()
@@ -121,19 +121,19 @@
         a, b = full.at[lo, cols(px)], full.at[hi, cols(py)]
         wait_in(a, in_recv.at[n, 0])
         move(n, a, a, 4, py)
-        move(n, a, a, 6, pc)
+        move(n, a, a, 7, pc)
         wait_in(b, in_recv.at[n, 2])
         move(n, b, b, 5, px)
-        move(n, b, b, 6, pc)
+        move(n, b, b, 7, pc)
 
     def plane_rest(n, full, first, many=2):
         for rr, p, i in ((hi, px, 1), (lo, py, 3), (lo, pd, 4), (hi, pd, 5))[first:first + many]:
             ref = full.at[rr, cols(p)]
             wait_in(ref, in_recv.at[n, i])
-            move(n, ref, ref, 6, pc)
-
-    def plane_last(n, full):
-        wait_in(full.at[:, pl.ds(0, 4 * LANE)], in_recv.at[n, 6])
+            move(n, ref, ref, 7 if i < 4 else 8, pc)
+
+    def plane_last(n, full, group):
+        wait_in(full.at[:, pl.ds(0, WIDE if group == 7 else LANE)], in_recv.at[n, group])
 
     plane_first(0, x_in, x_all)
 
@@ -198,7 +198,8 @@
     for c in loc[3:5]:
         c.wait()
     wait_in(gain_all.at[:, pl.ds(0, 7 * LANE)], g_recv.at[0])
-    plane_last(0, x_all)
+    for group in range(6, 9):
+        plane_last(0, x_all, group)
 
     def norm(xf):
         d = xf.shape[1]
@@ -217,13 +218,18 @@
         return pl.ds(pl.multiple_of(p * rows, rows), rows)
 
     def piece(p):
-        return pl.ds(p * ROWS, ROWS)
+        if p < 4:
+            return pl.ds(p * ROWS, ROWS), slice(None)
+        return pl.ds(WIDE, LANE), cols(lax.div(peer(2 * p - N_T), 2), WIDE)
+
+    def part(ref, i, p):
+        return ref.at[(i, *piece(p))]
 
     def sum_copy(src, dst, sl, p, device):
         return rcopy(src, dst, sum_send.at[sl], sum_recv.at[sl, p], (device, t))
 
     def from_end(q, k, p):
-        return sum_copy(dw.at[k, piece(p)], outs.at[q, piece(p)], q, p, inner)
+        return sum_copy(part(dw, k, p), part(outs, q, p), q, p, inner)
 
     def end_send(q, k, pieces):
         @pl.when(is_end)
@@ -261,10 +267,17 @@
 
     def grad_down(k):
         def grad(n, c):
-            nn = cols(n, WIDE)
-            dw[k, WIDE:, nn] = dot(act_t[...], dy_all[:, nn])
+            grad_down_at(k, n)
             return c
         lax.fori_loop(0, n_cols, grad, 0)
+
+    def grad_down_at(k, n):
+        nn = cols(n, WIDE)
+        dw[k, WIDE:, nn] = dot(act_t[...], dy_all[:, nn])
+
+    def first_down(p):
+        grad_down_at(c_mid2, lax.div(peer(2 * p - N_T), 2))
+        end_send(0, c_mid2, (p,))
 
     def backward_chunk(i, k):
         def tile(j, c):
@@ -298,31 +311,35 @@
     def _():
         hop_two()
 
-    forward_chunk(0, c_mid, 0)
+    forward_chunk(0, c_mid2, 1)
     plane_forward(1, dy_all)
-    forward_chunk(1, c_end, None)
+    turn_act(c_mid2)
+    loc[5].wait()
+    plane_last(1, dy_all, 6)
+    first_down(4)
+    forward_chunk(1, c_mid, 0)
 
     @pl.when(is_mid)
     def _():
         hop_three()
 
     plane_rest(1, dy_all, 0)
-    forward_chunk(2, c_mid2, 1)
-    turn_act(c_mid2)
+    forward_chunk(2, c_end, None)
+    plane_last(1, dy_all, 7)
+    first_down(5)
+    first_down(6)
     plane_rest(1, dy_all, 2)
-    loc[5].wait()
-    plane_last(1, dy_all)
+    plane_last(1, dy_all, 8)
     wait_sent(x_all.at[:, pl.ds(0, 7 * LANE)], in_send.at[0])
-    grad_down(c_mid2)
-    end_send(0, c_mid2, PIECE_ORDER[:2])
-    forward_chunk(3, c_end2, 2)
+    first_down(7)
 
     @pl.when(is_end)
     def _():
         wait_in(w2.at[cols(c_mid2), :], wz_end.at[1, 1])
 
-    backward_chunk(2, c_mid2)
-    end_send(0, c_mid2, PIECE_ORDER[2:])
+    backward_chunk(0, c_mid2)
+    end_send(0, c_mid2, PIECE_ORDER[4:])
+    forward_chunk(3, c_end2, 2)
 
     @pl.when(is_end)
     def _():
@@ -333,10 +350,10 @@
         def body(j, c):
             fx, fy = 1 - lax.div(j, 2), 1 - lax.rem(j, 2)
             i = fx + 2 * fy
-            away[i] = make(block(pc + fx * flips[1] + fy * flips[2]))
+            make(away, i, pc + fx * flips[1] + fy * flips[2], False)
             rcopy(away.at[i], r0.at[i], red_send.at[base // 10], red_recv.at[base + i], (z, pc)).start()
             return c
-        lax.fori_loop(0, 4, body, 0)
+        lax.fori_loop(0, N_T // 2, body, 0)
 
     def rsend(src, dst, group, sl, device):
         rcopy(src, dst, red_send.at[group], red_recv.at[sl], device).start()
@@ -344,12 +361,11 @@
     def rarrived(dst, sl):
         wait_in(dst, red_recv.at[sl])
 
-    a_half, b_half = pl.ds(0, hr), pl.ds(hr, hr)
-
     def stage1(r0, r1, make, base, between):
+        a_half, b_half = halves(r0)
         for i in (3, 1, 2, 0):
             rarrived(r0.at[i], base + i)
-            r0[i] += make(block((t, px, py, pd)[i]))
+            make(r0, i, (t, px, py, pd)[i], True)
             if i == 3:
                 rsend(r0.at[3, a_half], r1.at[0], base // 10, base + 4, (z, px))
                 rsend(r0.at[3, b_half], r1.at[1], base // 10, base + 5, (z, py))
@@ -360,106 +376,123 @@
             for p in between.get(i, ()):
                 pass_in(0, c_mid2, p)
 
+    def halves(r0):
+        n = r0.shape[1] // 2
+        return pl.ds(0, n), pl.ds(n, n)
+
     def stage2(r0, r1, r2, base):
+        a_half, b_half = halves(r0)
         rarrived(r1.at[0], base + 4)
-        r0[2, 0:hr] += r1[0]
+        r0[2, a_half] += r1[0]
         rsend(r0.at[2, a_half], r2.at[0], base // 10, base + 8, (z, py))
         rarrived(r1.at[1], base + 5)
-        r0[1, hr:rows] += r1[1]
+        r0[1, b_half] += r1[1]
         rsend(r0.at[1, b_half], r2.at[1], base // 10, base + 9, (z, px))
 
     def stage3(r0, r1, base):
-        rarrived(r1.at[2], base + 6)
-        r0[0, 0:hr] += r1[2]
-        rarrived(r1.at[3], base + 7)
-        r0[0, hr:rows] += r1[3]
+        for n, part in enumerate(halves(r0)):
+            rarrived(r1.at[2 + n], base + 6 + n)
+            r0[0, part] += r1[2 + n]
 
     def stage4(r0, r2, base):
-        rarrived(r2.at[0], base + 8)
-        r0[0, 0:hr] += r2[0]
-        rarrived(r2.at[1], base + 9)
-        r0[0, hr:rows] += r2[1]
-
-    def make_m(rr):
-        return dot(act[rr, :], w2[...])
-
-    def make_dh(rr):
-        return dot_cols(duv[rr, :], w13[...])
-
-    def finish(src, p):
+        for n, part in enumerate(halves(r0)):
+            rarrived(r2.at[n], base + 8 + n)
+            r0[0, part] += r2[n]
+
+    def make_m(ref, i, p, add):
+        def tile(j, c):
+            rr = cols(j, half)
+            out = dot(act[rr, :], w2[:, cols(p)])
+            ref[i, rr, :] = ref[i, rr, :] + out if add else out
+            return c
+        lax.fori_loop(0, 2, tile, 0)
+
+    def make_dh(ref, i, p, add):
+        out = dot_cols(duv[block(p), :], w13[...])
+        ref[i] = ref[i] + out if add else out
+
+    def finish(ref, i, p):
+        rr, _ = piece(p)
+        base = 2 * p - N_T
         for s in ORDER:
-            q = peer(s)
-            rcopy(src.at[:, cols(q)], dw_out.at[t, piece(p)], fin_sem.at[0], fin_sem.at[1], (z, q)).start()
-        pltpu.make_async_copy(src.at[:, cols(t)], dw_out.at[t, piece(p)], fin_sem.at[2]).start()
+            if p < 4 or s - s % 2 == base:
+                rcopy(ref.at[i, rr, cols(peer(s))], dw_out.at[t, rr], fin_sem.at[0], fin_sem.at[1], (z, peer(s))).start()
+        if base <= 0:
+            pltpu.make_async_copy(ref.at[i, rr, cols(t)], dw_out.at[t, rr], fin_sem.at[2]).start()
 
     def pass_in(q, k, p):
         @pl.when(is_mid)
         def _():
-            ref = outs.at[q, piece(p)]
+            ref = part(outs, q, p)
             sum_copy(ref, ref, q, p, outer).wait_recv()
-            outs[q, piece(p)] += dw[k, piece(p)]
-            sum_copy(ref, ins.at[q, piece(p)], 3 + q, p, inner).start()
+            outs[(q, *piece(p))] += dw[(k, *piece(p))]
+            sum_copy(ref, part(ins, q, p), 3 + q, p, inner).start()
 
     def pass_out(p):
         @pl.when(is_mid)
         def _():
-            ref = ins.at[1, piece(p)]
+            ref = part(ins, 1, p)
             sum_copy(ref, ref, 4, p, inner).wait_recv()
-            ins[1, piece(p)] += dw[c_end, piece(p)]
+            ins[(1, *piece(p))] += dw[(c_end, *piece(p))]
             sum_copy(ref, ref, 5, p, outer).start()
 
     def last_mid(p):
         @pl.when(is_mid)
         def _():
-            a, b = outs.at[2, piece(p)], ins.at[0, piece(p)]
+            a, b = part(outs, 2, p), part(ins, 0, p)
             sum_copy(b, b, 3, p, inner).wait_recv()
             sum_copy(a, a, 2, p, outer).wait_recv()
-            rr = piece(p)
-            outs[2, rr] += ins[0, rr] + dw[c_mid, rr]
-            finish(a, p)
+            outs[(2, *piece(p))] += ins[(0, *piece(p))] + dw[(c_mid, *piece(p))]
+            finish(outs, 2, p)
 
     def last_end(p):
         @pl.when(is_end)
         def _():
-            a = ins.at[1, piece(p)]
+            a = part(ins, 1, p)
             sum_copy(a, a, 5, p, inner).wait_recv()
-            rr = piece(p)
-            ins[1, rr] += dw[c_end, rr]
-            finish(a, p)
+            ins[(1, *piece(p))] += dw[(c_end, *piece(p))]
+            finish(ins, 1, p)
 
     stage0(m_away, m0, make_m, 0)
-    stage1(m0, m1, make_m, 0, {3: PIECE_ORDER[:1], 2: PIECE_ORDER[1:2]})
+    stage1(m0, m1, make_m, 0, {3: PIECE_ORDER[:1], 2: PIECE_ORDER[1:4]})
     turn_act(c_end2)
     grad_down(c_end2)
-    pass_in(0, c_mid2, PIECE_ORDER[2])
+    pass_in(0, c_mid2, 0)
     backward_chunk(3, c_end2)
     end_send(1, c_end2, PIECE_ORDER)
     turn_act(c_mid)
     grad_down(c_mid)
-    pass_in(0, c_mid2, PIECE_ORDER[3])
-    backward_chunk(0, c_mid)
+    pass_in(0, c_mid2, 1)
+    backward_chunk(1, c_mid)
     end_send(2, c_mid, PIECE_ORDER)
+    pass_in(0, c_mid2, 2)
+    pass_in(0, c_mid2, 3)
     stage2(m0, m1, m2, 0)
-    pass_in(0, c_mid2, PIECE_ORDER[4])
     turn_act(c_end)
     grad_down(c_end)
-    backward_chunk(1, c_end)
-    pass_in(0, c_mid2, PIECE_ORDER[5])
+    backward_chunk(2, c_end)
+    for p in PIECE_ORDER[:3]:
+        pass_in(1, c_end2, p)
     stage0(e_away, e0, make_dh, 10)
+    pass_in(1, c_end2, PIECE_ORDER[3])
     stage1(e0, e1, make_dh, 10, {})
+
+    def put(src, dst, local):
+        c = pltpu.make_async_copy(src, dst, local_sem.at[local])
+        c.start()
+        loc.append(c)
 
     def spread(src, dst, group, local):
         for s in ORDER:
             q = peer(s)
             rsend(src.at[:, cols(q)], dst.at[block(t), :], group, group + 18, (z, q))
-        c = pltpu.make_async_copy(src.at[:, cols(t)], dst.at[block(t), :], local_sem.at[local])
-        c.start()
-        loc.append(c)
+        put(src.at[:, cols(t)], dst.at[block(t), :], local)
 
     def make_y():
         stage4(m0, m2, 0)
-        y_rows[...] = (x_rows[...].astype(F32) + m0[0]).astype(BF16)
-        spread(y_rows, y_out, 2, 6)
+        loc[6].wait()
+        x_own[...] = (x_own[...].astype(F32) + m0[0]).astype(BF16)
+        put(x_own, y_out, 6)
 
     def make_dx():
         stage4(e0, e2, 10)
@@ -470,11 +503,11 @@
         e_mean = jnp.sum(e, axis=1, keepdims=True) / d
         ex_mean = jnp.sum(e * xhat, axis=1, keepdims=True) / d
         dy_rows = dy_all[block(t), :].astype(F32)
-        dx_rows[...] = (dy_rows + r * (e - e_mean - xhat * ex_mean)).astype(BF16)
+        x_rows[...] = (dy_rows + r * (e - e_mean - xhat * ex_mean)).astype(BF16)
         dg_rows[...] = jnp.sum((dh * xhat).reshape(rows // 8, 8, d), axis=0)
         for s in ORDER:
             rsend(dg_rows.at[:, cols(peer(s))], dg_plane.at[s - 1], 4, 22, (z, peer(s)))
-        spread(dx_rows, dx_out, 3, 7)
+        spread(x_rows, dx_out, 3, 7)
 
     def gain_plane():
         total = dg_rows[:, cols(t)]
@@ -490,34 +523,37 @@
         parts = [dg_line[lax.rem(z - s + 4, 4)] for s in range(4)]
         dg_out[...] = sum(parts[1:], parts[0])
 
-    per = 33.7 / PIECES
-    plan = [(84, lambda: stage3(m0, m1, 0)), (108.6, make_y),
-            (108.5, lambda: stage2(e0, e1, e2, 10)), (121, lambda: stage3(e0, e1, 10)),
-            (131, make_dx), (149.5, gain_plane), (157, gain_line)]
-    for n, p in enumerate(PIECE_ORDER):
-        done = 86 + per * (n + 1)
-        plan.append((done, lambda p=p: pass_in(1, c_end2, p)))
-        plan.append((done + per + 1, lambda p=p: pass_out(p)))
-        plan.append((done + 2 * per + 2, lambda p=p: last_end(p)))
+    plan = [(84, lambda: stage3(m0, m1, 0)), (96, make_y),
+            (109, lambda: stage2(e0, e1, e2, 10)), (120, lambda: stage3(e0, e1, 10)),
+            (131, make_dx), (147, gain_plane), (157, gain_line)]
+    done = 78.4
+    for p in PIECE_ORDER:
+        done += 5.6 if p < 4 else 2.8
+        if p < 4:
+            plan.append((done, lambda p=p: pass_in(1, c_end2, p)))
+        late = max(done, 89.6)
+        plan.append((late + 6.6, lambda p=p: pass_out(p)))
+        plan.append((late + 13, lambda p=p: last_end(p)))
         plan.append((done + 33.7, lambda p=p: last_mid(p)))
     for _, fn in sorted(plan, key=lambda e: e[0]):
         fn()
 
     seven = pl.ds(0, 7 * LANE)
-    rarrived(y_out.at[pl.ds(0, 7 * rows), :], 20)
     rarrived(dx_out.at[pl.ds(0, 7 * rows), :], 21)
     wait_in(dw_out.at[pl.ds(0, 7)], fin_sem.at[1])
     pltpu.make_async_copy(dw_out.at[0], dw_out.at[0], fin_sem.at[2]).wait()
-    for c in loc[6:]:
+    for c in loc[7:]:
         c.wait()
     wait_sent(dw_out.at[pl.ds(0, 7)], fin_sem.at[0])
     for n in range(3):
         wait_sent(w13.at[pl.ds(0, LANE), seven], w_send.at[n])
     wait_sent(gain_all.at[:, seven], w_send.at[3])
     wait_sent(dy_all.at[:, seven], in_send.at[1])
-    for n, ref in enumerate((uv_all.at[pl.ds(0, 7)], uv_all.at[pl.ds(0, 7)], y_rows.at[:, seven], dx_rows.at[:, seven],
+    most = uv_all.at[pl.ds(0, 7)]
+    for n, ref in enumerate((most, most, None, x_rows.at[:, seven],
                              dg_rows.at[:, seven], dg_line.at[pl.ds(1, 3)])):
-        wait_sent(ref, red_send.at[n])
+        if ref is not None:
+            wait_sent(ref, red_send.at[n])
 
     def chunk_sent(sl):
         wait_sent(w13.at[:, cols(0, WIDE)], wz_send.at[sl, 0])
@@ -560,7 +596,9 @@
         s = jax.ShapeDtypeStruct
         V = pltpu.VMEM
         dma = pltpu.SemaphoreType.DMA
-        red = [V((4, rows, d), F32), V((4, rows, d), F32), V((4, rows // 2, d), F32), V((2, rows // 2, d), F32)]
+        def red(r, c):
+            half = V((2, r // 2, c), F32)
+            return [V((4, r, c), F32), V((4, r // 2, c), F32), half]
         y, dx, dw, dg = pl.pallas_call(
             step_kernel,
             out_shape=(s((tokens, lane), BF16), s((tokens, lane), BF16), s((N_T, CHUNK, lane), F32), s((8, lane), F32)),
@@ -569,12 +607,12 @@
             scratch_shapes=[
                 V((tokens, d), BF16), V((tokens, d), BF16), V((tokens, d), BF16), V((1, d), F32),
                 V((d, 2 * f), BF16), V((f, d), BF16), V((tokens, f), BF16), V((lane, tokens), BF16),
-                V((WIDE, tokens), BF16), V((N_Z, CHUNK, d), F32), V((N_T, rows, d), F32)] + red + red[1:] + [
+                V((WIDE, tokens), BF16), V((N_Z, CHUNK, d), F32), V((N_T, rows, d), F32), V((4, tokens, lane), F32)] + red(tokens, lane) + red(rows, d) + [
                 V((3, CHUNK, d), F32), V((2, CHUNK, d), F32),
-                V((rows, d), BF16), V((rows, d), BF16), V((rows, d), BF16), V((8, d), F32),
+                V((rows, d), BF16), V((tokens, lane), BF16), V((8, d), F32),
                 V((7, 8, lane), F32), V((4, 8, lane), F32),
-                dma((4,)), dma((N_T, 2)), dma((1,)), dma((2,)), dma((2, 7)), dma((6, 2)), dma((3, 2)),
-                dma((3, N_T // 2, 2)), dma((6,)), dma((6, PIECES)), dma((3,)), dma((6,)), dma((24,)), dma((8,))],
+                dma((4,)), dma((N_T, 2)), dma((1,)), dma((2,)), dma((2, 9)), dma((6, 2)), dma((3, 2)),
+                dma((3, N_T // 2, 2)), dma((6,)), dma((6, PIECES)), dma((3,)), dma((6,)), dma((24,)), dma((9,))],
             compiler_params=pltpu.CompilerParams(collective_id=0, has_side_effects=True, vmem_limit_bytes=67043328),
             name="step",
         )(x_blk, dy_blk, gain_blk[None, :], w1_blk, w3_blk, w2_blk)

time: 169 us -> 163 us (0.964)
  Pallas kernels: 168 us -> 162 us
    pallas_call x1, Pallas kernels: 164 us -> 158 us  [local_step(): pl.pallas_call(step_kernel, out_shape=(s((tokens, lane), BF16), s((tokens...]
where the time goes in v6:
time: 163 us; the launch traced here: 162 us
  Pallas kernels  162 us (99%)
    pallas_call x1, Pallas kernels, local_step(): pl.pallas_call(step_kernel, out_shape=(s((tokens, lane), BF16), s((tokens...  158 us
    pallas_call x1, Pallas kernels, local_step(): pl.pallas_call(place_kernel, out_shape=(s((tokens, lane), BF16), s((token...  3.52 us

profile of v6, /device:TPU:0, one launch (start us, length us, event | category | flops | bytes accessed | tf_op | source)
XLA Modules:
  0.0 162.4 jit_solution(558963854390909701)
XLA Ops:
  0.6 158.2 %step.1 = (bf16[2048,128]{1,0:T(8,128)(2,1)}, bf16[2048,128]{1,0:T(8,128)(2,1)}, f32[8,384,128]{2,1,0:T(8,128)}, f32[8,128]{1,0:T(8,128)}) custom-call(bf16[2048,128]{1,0:T(8,128)(2,1)} %x_in.1, bf16[2048,128]{1,0:T(8,128)(2,1)} %dy_in.1, f32[1,128]{1,0:T(1,128)} %bitcast.2, bf16[128,1024]{1,0:T(8,128)(2,1)} %w1_in.1, bf16[128,1024]{1,0:T(8,128)(2,1)} %w3_in.1, ...), custom_call_target="tpu_custom_call" | custom-call | tf_op jit(solution)/shard_map/step/pallas_call | solution.py:602
  158.9 3.5 %place.1 = (bf16[2048,128]{1,0:T(8,128)(2,1)}, bf16[2048,128]{1,0:T(8,128)(2,1)}, f32[128,1024]{1,0:T(8,128)}, f32[128,1024]{1,0:T(8,128)}, f32[1024,128]{1,0:T(8,128)}, /*index=5*/f32[1,128]{1,0:T(1,128)}) custom-call(bf16[2048,128]{1,0:T(8,128)(2,1)} %get-tuple-element.16.y_in, bf16[2048,128]{1,0:T(8,128)(2,1)} %get-tuple-element.17.dx_in, ...), custom_call_target="tpu_custom_call" | custom-call | tf_op jit(solution)/shard_map/place/pallas_call | solution.py:620

commit v7 on v6

--- a/solution.py
+++ b/solution.py
@@ -337,15 +337,6 @@
     def _():
         wait_in(w2.at[cols(c_mid2), :], wz_end.at[1, 1])
 
-    backward_chunk(0, c_mid2)
-    end_send(0, c_mid2, PIECE_ORDER[4:])
-    forward_chunk(3, c_end2, 2)
-
-    @pl.when(is_end)
-    def _():
-        wait_in(w2.at[cols(c_mid), :], wz_end.at[0, 1])
-        wait_in(w2.at[cols(c_end2), :], wz_end.at[2, 1])
-
     def stage0(away, r0, make, base):
         def body(j, c):
             fx, fy = 1 - lax.div(j, 2), 1 - lax.rem(j, 2)
@@ -400,12 +391,8 @@
             r0[0, part] += r2[n]
 
     def make_m(ref, i, p, add):
-        def tile(j, c):
-            rr = cols(j, half)
-            out = dot(act[rr, :], w2[:, cols(p)])
-            ref[i, rr, :] = ref[i, rr, :] + out if add else out
-            return c
-        lax.fori_loop(0, 2, tile, 0)
+        out = dot(act[...], w2[:, cols(p)])
+        ref[i] = ref[i] + out if add else out
 
     def make_dh(ref, i, p, add):
         out = dot_cols(duv[block(p), :], w13[...])
@@ -453,8 +440,21 @@
             ins[(1, *piece(p))] += dw[(c_end, *piece(p))]
             finish(ins, 1, p)
 
-    stage0(m_away, m0, make_m, 0)
-    stage1(m0, m1, make_m, 0, {3: PIECE_ORDER[:1], 2: PIECE_ORDER[1:4]})
+    def start_m():
+        forward_chunk(3, c_end2, 2)
+
+        @pl.when(is_end)
+        def _():
+            wait_in(w2.at[cols(c_mid), :], wz_end.at[0, 1])
+            wait_in(w2.at[cols(c_end2), :], wz_end.at[2, 1])
+
+        stage0(m_away, m0, make_m, 0)
+        stage1(m0, m1, make_m, 0, {3: PIECE_ORDER[:1], 2: PIECE_ORDER[1:4]})
+
+    pl.when(is_mid)(start_m)
+    backward_chunk(0, c_mid2)
+    end_send(0, c_mid2, PIECE_ORDER[4:])
+    pl.when(is_end)(start_m)
     turn_act(c_end2)
     grad_down(c_end2)
     pass_in(0, c_mid2, 0)
@@ -524,8 +524,8 @@
         dg_out[...] = sum(parts[1:], parts[0])
 
     plan = [(84, lambda: stage3(m0, m1, 0)), (96, make_y),
-            (109, lambda: stage2(e0, e1, e2, 10)), (120, lambda: stage3(e0, e1, 10)),
-            (131, make_dx), (147, gain_plane), (157, gain_line)]
+            (101.9, lambda: stage2(e0, e1, e2, 10)), (120, lambda: stage3(e0, e1, 10)),
+            (123, make_dx), (147, gain_plane), (157, gain_line)]
     done = 78.4
     for p in PIECE_ORDER:
         done += 5.6 if p < 4 else 2.8

time: 163 us -> 161 us (0.988)
  no operation moved by 1% of the time
where the time goes in v7:
time: 161 us
  Pallas kernels  161 us (100%)
    pallas_call x1, Pallas kernels, local_step(): pl.pallas_call(step_kernel, out_shape=(s((tokens, lane), BF16), s((tokens...  157 us
    pallas_call x1, Pallas kernels, local_step(): pl.pallas_call(place_kernel, out_shape=(s((tokens, lane), BF16), s((token...  3.52 us

profile of v7, /device:TPU:0, one launch (start us, length us, event | category | flops | bytes accessed | tf_op | source)
XLA Modules:
  0.0 161.3 jit_solution(11970160001776978281)
XLA Ops:
  0.6 157.2 %step.1 = (bf16[2048,128]{1,0:T(8,128)(2,1)}, bf16[2048,128]{1,0:T(8,128)(2,1)}, f32[8,384,128]{2,1,0:T(8,128)}, f32[8,128]{1,0:T(8,128)}) custom-call(bf16[2048,128]{1,0:T(8,128)(2,1)} %x_in.1, bf16[2048,128]{1,0:T(8,128)(2,1)} %dy_in.1, f32[1,128]{1,0:T(1,128)} %bitcast.2, bf16[128,1024]{1,0:T(8,128)(2,1)} %w1_in.1, bf16[128,1024]{1,0:T(8,128)(2,1)} %w3_in.1, ...), custom_call_target="tpu_custom_call" | custom-call | tf_op jit(solution)/shard_map/step/pallas_call | solution.py:602
  157.8 3.5 %place.1 = (bf16[2048,128]{1,0:T(8,128)(2,1)}, bf16[2048,128]{1,0:T(8,128)(2,1)}, f32[128,1024]{1,0:T(8,128)}, f32[128,1024]{1,0:T(8,128)}, f32[1024,128]{1,0:T(8,128)}, /*index=5*/f32[1,128]{1,0:T(1,128)}) custom-call(bf16[2048,128]{1,0:T(8,128)(2,1)} %get-tuple-element.16.y_in, bf16[2048,128]{1,0:T(8,128)(2,1)} %get-tuple-element.17.dx_in, ...), custom_call_target="tpu_custom_call" | custom-call | tf_op jit(solution)/shard_map/place/pallas_call | solution.py:620
